TPU v7x, 32 devices: a whole 2x2x4 slice. The times are simulated.
32 devices in a mesh: batch: 4 (over z), seq: 8 (over y, x, core).
Axes of the slice: x: 2, y: 2, z: 4, core: 2. Of those that a mesh axis runs over, the one named last changes fastest.
Arguments:
- hidden: bfloat16 [4, 4096, 4096], P('batch', 'seq'), may hold values from -6 to 6
- score_direction: bfloat16 [4, 4096, 4096], P('batch', 'seq'), may hold values from -6 to 6
- adapter_down: bfloat16 [4096, 256], replicated, may hold values from -0.09375 to 0.09375
- adapter_up: bfloat16 [4096, 256], replicated, may hold values from -0.09375 to 0.09375
- rewards: float32 [4, 4096], P('batch', 'seq'), may hold values from -0.3125 to 0.3125
- values: float32 [4, 4096], P('batch', 'seq'), may hold values from -120 to 120
- log_ratio: float32 [4, 4096], P('batch', 'seq'), may hold values from -4 to 4
- lengths: int32 [4], P('batch'), may hold values from 1024 to 4096
Outputs:
- returns: float32 [4, 4096], P('batch', 'seq')
- grad_down: float32 [4096, 256], P(('batch', 'seq'))
- grad_up: float32 [4096, 256], P(('batch', 'seq'))
All inputs are finite; a program needn't handle non-finite values.
Results may differ from a plain program's by a relative error of at most 0.0029.
Values sent between devices are 32-bit elements; how exact they have to be, the bound alone decides.
No kernel may reach another device: no remote copies, remote signals or barrier semaphores. Data moves between devices by JAX's collectives and lax.ppermute only.
A program may use at most 128 MiB of HBM per device.

v0:
```python
import functools
import math

import jax
import jax.numpy as jnp
from jax import lax
from jax.experimental import pallas as pl
from jax.experimental.pallas import tpu as pltpu
from jax.sharding import PartitionSpec as P


ratio_cap = 2.0
weight_gain = 0.08
AXES = ("batch", "seq")
LANES = 128
KERNEL_VMEM = 8 * 1024 * 1024
F32 = jnp.float32

PARTS = (("xzy", 12), ("yxz", 12), ("zyx", 12), ("yxz", 15), ("xyz", 13))
TURNS = (0, 2, 1, 4, 0, 3, 1, 4, 2, 0, 3, 4, 1, 3, 2)

SMEM = pl.BlockSpec(memory_space=pltpu.SMEM)
VMEM = pl.BlockSpec(memory_space=pltpu.VMEM)
HBM = pl.BlockSpec(memory_space=pltpu.HBM)


def swap(x, mask, count):
    return lax.ppermute(x, AXES, [(i, i ^ mask) for i in range(count)])


class Line:
    def __init__(self):
        self.token = None

    def call(self, body, outs, ins, scalars=(), from_hbm=(), scratch=(), in_vmem=True):
        first = self.token is None
        n_in = len(scalars) + len(from_hbm) + len(ins)

        def run(*refs):
            given, refs = refs[:n_in], refs[n_in:]
            if not first:
                refs = refs[1:]
            made, token, rest = refs[: len(outs)], refs[len(outs)], refs[len(outs) + 1 :]
            body(*given, *made, *rest)
            token[...] = jnp.zeros_like(token)

        kind = pltpu.VMEM if in_vmem else jax.ShapeDtypeStruct
        tokens = [] if first else [self.token]
        kernel = pl.pallas_call(
            run,
            out_shape=(*[kind(*o) for o in outs], pltpu.VMEM((8, LANES), F32)),
            in_specs=[SMEM] * len(scalars) + [HBM] * len(from_hbm) + [VMEM] * (len(ins) + len(tokens)),
            out_specs=(VMEM,) * (len(outs) + 1),
            scratch_shapes=list(scratch),
            compiler_params=pltpu.CompilerParams(vmem_limit_bytes=KERNEL_VMEM),
        )
        from_hbm = [pltpu.with_memory_space_constraint(x, pltpu.HBM) for x in from_hbm]
        ins = [pltpu.with_memory_space_constraint(x, pltpu.VMEM) for x in [*ins, *tokens]]
        *got, self.token = kernel(*scalars, *from_hbm, *ins)
        return got


def row_of(tokens):
    return lax.broadcasted_iota(jnp.int32, (1, tokens), 1)


def first_body(length, rewards, live, group, *, total_len):
    tokens = rewards.shape[1]
    at = row_of(tokens)
    valid = jnp.where(at + lax.axis_index("seq") * tokens < length[0], 1.0, 0.0)
    row = rewards[...] * valid * jnp.exp(-at.astype(F32) / total_len)
    live[...] = row
    group[...] = jnp.broadcast_to(jnp.sum(row, axis=1, keepdims=True), group.shape)


def carry(group, other, carried, side, tokens, total_len):
    shard = lax.axis_index("seq")
    upper = jnp.full(group.shape, shard & side, jnp.int32) != 0
    steps = jnp.full(group.shape, side - 1 - (shard & (side - 1)), jnp.int32).astype(F32)
    here = jnp.where(upper, 0.0, jnp.exp(-steps * (tokens / total_len)))
    far = math.exp(-side * tokens / total_len)
    return jnp.where(upper, other + far * group, group + far * other), carried + here * other


def carry_body(group, other, carried, new_group, new_carried, **sizes):
    new_group[...], new_carried[...] = carry(group[...], other[...], carried[...], **sizes)


def project_body(src_hbm, mat_hbm, src, out_t, mat, acc, src_sems, mat_sems, *, steps):
    width = src.shape[1]
    step = width // steps
    copies = []
    for i in range(steps):
        cut = pl.ds(i * step, step)
        copies.append(pltpu.make_async_copy(src_hbm.at[:, cut], src.at[:, cut], src_sems.at[i]))
        copies.append(pltpu.make_async_copy(mat_hbm.at[cut, :], mat.at[cut, :], mat_sems.at[i]))
    for c in copies:
        c.start()
    for i in range(steps):
        copies[2 * i].wait()
        copies[2 * i + 1].wait()
        cut = slice(i * step, (i + 1) * step)
        part = jnp.dot(src[:, cut], mat[cut, :], preferred_element_type=F32)
        if i:
            part = part + acc[...]
        if i < steps - 1:
            acc[...] = part
        else:
            out_t[...] = part.T


def within_of(row, total_len):
    tokens = row.shape[1]
    first = row.astype(jnp.bfloat16)
    rest = row - first.astype(F32)
    second = rest.astype(jnp.bfloat16)
    third = (rest - second.astype(F32)).astype(jnp.bfloat16)
    rows = jnp.concatenate([first, second, third], axis=0)
    k_of = lax.broadcasted_iota(jnp.int32, (tokens, tokens), 0)
    t_of = lax.broadcasted_iota(jnp.int32, (tokens, tokens), 1)
    sums = jnp.dot(rows, (k_of >= t_of).astype(jnp.bfloat16), preferred_element_type=F32)
    return jnp.sum(sums, axis=0, keepdims=True) * jnp.exp(row_of(tokens).astype(F32) / total_len)


def within_body(row, within, *, total_len):
    within[...] = within_of(row[...], total_len)


def weigh_body(
    length, down_t, up_t, within, group, other, carried, values, log_ratio,
    returns, scaled_up, scaled_down, *, side, total_len, seq_total,
):
    rank, tokens = down_t.shape
    at = row_of(tokens)
    _, incoming = carry(group[...], other[...], carried[...], side, tokens, total_len)
    tail = jnp.exp((at - tokens).astype(F32) / total_len)
    back = within[...] + tail * incoming[0:1, 0:1]
    returns[...] = back
    adapter_scale = 1.0 / math.sqrt(rank)
    delta = adapter_scale * jnp.sum(down_t[...] * up_t[...], axis=0, keepdims=True)
    importance = jnp.exp(log_ratio[...] + delta)
    count = length[0]
    lens = jnp.full((1, tokens), count, jnp.int32).astype(F32)
    gain = weight_gain * math.sqrt(total_len * rank / seq_total) / lens
    valid = jnp.where(at + lax.axis_index("seq") * tokens < count, 1.0, 0.0)
    weight = -adapter_scale * (valid * jnp.minimum(importance, ratio_cap) * (back - values[...]) * gain)
    scaled_up[...] = (weight * up_t[...]).astype(jnp.bfloat16)
    scaled_down[...] = (weight * down_t[...]).astype(jnp.bfloat16)


def blocks_body(*refs, jobs, seq_size, n_out, adds):
    hid, direction, scaled_up, scaled_down = refs[:4]
    received = refs[4 : 4 + n_out] if adds else ()
    outs = refs[4 + n_out :] if adds else refs[4:]
    me = lax.axis_index("batch") * seq_size + lax.axis_index("seq")
    for out_at, tiles, row_at, rows, side, from_row in jobs:
        src, weight = ((hid, scaled_up), (direction, scaled_down))[side]
        out = outs[out_at]
        for i in range(0, len(tiles), 2):
            pair = tiles[i : i + 2]
            cols = [src[:, pl.ds(pl.multiple_of((t ^ me) * LANES, LANES), LANES)] for t in pair]
            block = jnp.concatenate(cols, axis=1) if len(cols) > 1 else cols[0]
            grad = jnp.dot(weight[from_row : from_row + rows, :], block, preferred_element_type=F32)
            for j in range(len(pair)):
                part = grad[:, j * LANES : (j + 1) * LANES]
                if adds:
                    part = part + received[out_at][i + j, row_at : row_at + rows, :]
                out[i + j, row_at : row_at + rows, :] = part


def blocks(line, ops, wanted, received, seq_size):
    jobs, shapes = [], []
    for out_at, (tiles, pieces) in enumerate(wanted):
        at = 0
        for side, from_row, rows in pieces:
            jobs.append((out_at, tuple(tiles), at, rows, side, from_row))
            at += rows
        shapes.append(((len(tiles), at, LANES), F32))
    extra = tuple(received) if received is not None else ()
    body = functools.partial(
        blocks_body, jobs=tuple(jobs), seq_size=seq_size, n_out=len(wanted), adds=received is not None
    )
    return line.call(body, shapes, (*ops, *extra))


def fold_body(keep, got, send, left):
    half = send.shape[0]
    send[...] = keep[half:] + got[half:]
    left[...] = keep[:half] + got[:half]


def total_body(*refs, n, rank):
    keeps, gots, (down, up, squares) = refs[:n], refs[n : 2 * n], refs[2 * n :]
    at, row = 0, 0.0
    for keep, got in zip(keeps, gots):
        part = keep[0] + got[0]
        row = row + jnp.sum(part * part, axis=0, keepdims=True)
        rows = part.shape[0]
        split = min(max(rank - at, 0), rows)
        if split:
            down[at : at + split, :] = part[:split]
        if split < rows:
            up[at + split - rank : at + rows - rank, :] = part[split:]
        at += rows
    squares[...] = jnp.broadcast_to(row[None], squares.shape)


def clip_body(down, up, squares, grad_down, grad_up, *, clip_norm):
    norm = jnp.sqrt(jnp.sum(jnp.sum(squares[...], axis=0), axis=1, keepdims=True))
    factor = clip_norm / jnp.maximum(norm, clip_norm)
    grad_down[...] = (down[...] * factor).T
    grad_up[...] = (up[...] * factor).T


def tiles_of(order, fixed):
    names = [fixed]
    for mask in order:
        names = [n | b for n in names for b in (0, mask)]
    return names


def log2(n):
    return n.bit_length() - 1


def turns_of(halvings):
    n = len(PARTS)
    return TURNS if len(TURNS) == n * (halvings - 1) else [i for _ in range(halvings - 1) for i in range(n)]


def local_blocks(hidden, score_direction, adapter_down, adapter_up, rewards, values, log_ratio, lengths):
    return in_blocks(hidden, score_direction, adapter_down, adapter_up, rewards, values, log_ratio, lengths)


def in_blocks(hidden, score_direction, adapter_down, adapter_up, rewards, values, log_ratio, lengths):
    _, tokens, width = hidden.shape
    rank = adapter_down.shape[1]
    nb, ns = lax.axis_size("batch"), lax.axis_size("seq")
    count = nb * ns
    total_len = tokens * ns
    hid_hbm, direction_hbm = hidden[0], score_direction[0]
    line = Line()

    bits = [1 << j for j in range(log2(ns))]
    tile = ((8, LANES), F32)
    live, group = line.call(
        functools.partial(first_body, total_len=total_len), [((1, tokens), F32), tile], (rewards,), (lengths,)
    )
    carried = jnp.zeros(*tile)
    steps = 8
    under = [(hid_hbm, adapter_down), (direction_hbm, adapter_up)]
    made = []
    for j, side in enumerate(bits):
        other = swap(group, side, count)
        if j == 0:
            (within,) = line.call(functools.partial(within_body, total_len=total_len), [((1, tokens), F32)], (live,))
        if j >= len(bits) - len(under):
            src, mat = under[len(made)]
            made.append(
                line.call(
                    functools.partial(project_body, steps=steps),
                    [((tokens, width), src.dtype), ((rank, tokens), F32)],
                    (),
                    from_hbm=(src, mat),
                    scratch=[
                        pltpu.VMEM((width, rank), mat.dtype),
                        pltpu.VMEM((tokens, rank), F32),
                        pltpu.SemaphoreType.DMA((steps,)),
                        pltpu.SemaphoreType.DMA((steps,)),
                    ],
                )
            )
        if j < len(bits) - 1:
            group, carried = line.call(
                functools.partial(carry_body, side=side, tokens=tokens, total_len=total_len),
                [tile, tile], (group, other, carried),
            )
    (hid, down_t), (direction, up_t) = made
    returns, scaled_up, scaled_down = line.call(
        functools.partial(weigh_body, side=bits[-1], total_len=total_len, seq_total=nb),
        [((1, tokens), F32), ((rank, tokens), jnp.bfloat16), ((rank, tokens), jnp.bfloat16)],
        (down_t, up_t, within, group, other, carried, values, log_ratio), (lengths,),
    )

    ops = (hid, direction, scaled_up, scaled_down)
    core, plane = bits[0], bits[1:]
    masks = {"x": plane[: len(plane) // 2], "y": plane[len(plane) // 2 :], "z": [ns << j for j in range(log2(nb))]}
    orders, pieces, at = [], [], 0
    for axes, share in PARTS:
        orders.append([m for axis in axes for m in masks[axis]])
        end = at + 2 * rank * share // 64
        pieces.append([
            (side, max(at - side * rank, 0), min(end, rank * (side + 1)) - max(at, rank * side))
            for side in (0, 1)
            if min(end, rank * (side + 1)) > max(at, rank * side)
        ])
        at = end
    n = len(PARTS)
    sends = [(tiles_of(orders[i][1:], orders[i][0]), pieces[i]) for i in range(n)]
    stays = [(tiles_of(orders[i][1:], 0), pieces[i]) for i in range(n)]
    far = lambda w: ([t | core for t in w[0]], w[1])
    got, sent, theirs = [None] * n, [None] * n, [None] * n
    for i in range(n + 1):
        if i < n:
            (theirs[i],) = blocks(line, ops, [far(sends[i])], None, ns)
            got[i] = swap(theirs[i], core, count)
        if i:
            (mine,) = blocks(line, ops, [sends[i - 1]], [got[i - 1]], ns)
            sent[i - 1] = swap(mine, orders[i - 1][0], count)
    got = [swap(t, core, count) for t in blocks(line, ops, [far(w) for w in stays], None, ns)]
    kept = blocks(line, ops, stays, got, ns)

    taken = [1] * n
    for i in turns_of(len(orders[0])):
        blocks_now, rows, _ = kept[i].shape
        send, kept[i] = line.call(fold_body, [((blocks_now // 2, rows, LANES), F32)] * 2, (kept[i], sent[i]))
        sent[i] = swap(send, orders[i][taken[i]], count)
        taken[i] += 1

    down, up, squares = line.call(
        functools.partial(total_body, n=n, rank=rank),
        [((rank, LANES), F32), ((rank, LANES), F32), ((count, 1, LANES), F32)], (*kept, *sent),
    )
    squares = lax.all_to_all(squares, AXES, 0, 0, tiled=True)
    clip_norm = 0.5 * math.sqrt(2.0 * width * rank)
    grad_down, grad_up = line.call(
        functools.partial(clip_body, clip_norm=clip_norm), [((LANES, rank), F32)] * 2, (down, up, squares), in_vmem=False
    )
    return returns, grad_down, grad_up


def local_plain(hidden, score_direction, adapter_down, adapter_up, rewards, values, log_ratio, lengths):
    seq_count, shard_len, model_width = hidden.shape
    rank = adapter_down.shape[1]
    ns = lax.axis_size("seq")
    total_len = shard_len * ns
    seq_total = seq_count * lax.axis_size("batch")
    shard = lax.axis_index("seq")
    inner = jnp.arange(shard_len, dtype=jnp.int32)
    valid = ((shard * shard_len + inner)[None, :] < lengths[:, None]).astype(F32)
    scale = 1.0 / math.sqrt(rank)
    down = jnp.einsum("ogz,zw->ogw", hidden, adapter_down, preferred_element_type=F32)
    up = jnp.einsum("ogz,zw->ogw", score_direction, adapter_up, preferred_element_type=F32)
    importance = jnp.exp(log_ratio + scale * jnp.sum(down * up, axis=-1))
    live = rewards * valid
    offsets = (inner[None, :] - inner[:, None]).astype(F32)
    discount = jnp.where(offsets >= 0, jnp.exp(-offsets / total_len), jnp.zeros_like(offsets))
    within = jnp.einsum("sk,tk->st", live, discount, precision=lax.Precision.HIGHEST)
    firsts = lax.all_gather(within[:, :1], "seq", axis=1, tiled=True)
    index = jnp.arange(ns, dtype=jnp.int32)
    steps = (index - shard - 1).astype(F32)
    here = jnp.where(index > shard, jnp.exp(-steps * shard_len / total_len), jnp.zeros_like(steps))
    carried = jnp.sum(firsts * here[None, :], axis=1)
    tail = jnp.exp(-(shard_len - inner).astype(F32) / total_len)
    returns = within + tail[None, :] * carried[:, None]
    gain = weight_gain * math.sqrt(total_len * rank / seq_total) / lengths.astype(F32)
    weight = valid * jnp.minimum(importance, ratio_cap) * (returns - values) * gain[:, None]
    scaled_up = (-scale * weight[:, :, None] * up).astype(jnp.bfloat16)
    scaled_down = (-scale * weight[:, :, None] * down).astype(jnp.bfloat16)
    terms = jnp.concatenate(
        [
            jnp.einsum("oxe,oxq->eq", hidden, scaled_up, preferred_element_type=F32),
            jnp.einsum("oxe,oxq->eq", score_direction, scaled_down, preferred_element_type=F32),
        ],
        axis=1,
    )
    own = lax.psum_scatter(terms, AXES, scatter_dimension=0, tiled=True)
    norm = jnp.sqrt(lax.psum(jnp.sum(own * own), AXES))
    clip_norm = 0.5 * math.sqrt(2.0 * model_width * rank)
    factor = clip_norm / jnp.maximum(norm, clip_norm)
    return returns, own[:, :rank] * factor, own[:, rank:] * factor


def solution(mesh):
    placed = (
        P("batch", "seq", None),
        P("batch", "seq", None),
        P(),
        P(),
        P("batch", "seq"),
        P("batch", "seq"),
        P("batch", "seq"),
        P("batch"),
    )
    nb, ns = mesh.shape["batch"], mesh.shape["seq"]

    def step(hidden, *rest):
        powers = nb & (nb - 1) == 0 and ns & (ns - 1) == 0 and nb >= 2 and ns >= 8
        blocked = powers and hidden.shape[0] == nb and hidden.shape[2] == nb * ns * LANES
        return jax.shard_map(
            local_blocks if blocked else local_plain,
            mesh=mesh,
            in_specs=placed,
            out_specs=(P("batch", "seq"), P(AXES, None), P(AXES, None)),
            check_vma=False,
        )(hidden, *rest)

    return step
```

profile of v0, /device:TPU:0, one launch (start us, length us, event | category | flops | bytes accessed | tf_op | source)
XLA Modules:
  0.0 102.2 jit_solution(9895872797666967422)
XLA Ops:
  1.3 0.7 copy-done.2
  2.1 0.5 collective-permute-start
  2.8 0.6 collective-permute-done.refs_1_
  3.4 2.9 %collective-permute-start.1 = (f32[8,128]{1,0:T(8,128)S(1)}, f32[8,128]{1,0:T(8,128)S(1)}, u32[]{:S(2)}, u32[]{:S(2)}) collective-permute-start(f32[8,128]{1,0:T(8,128)S(1)} %get-tuple-element.113.refs_0_), channel_id=1, source_target_pairs={{0,2},{1,3},{2,0},{3,1},{4,6},{5,7},{6,4},{7,5},{8,10},{9,11},{10,... | collective-permute-start | bytes 12296 | tf_op jit(solution)/shard_map/ppermute | solution.py:28
  6.3 4.0 %shard_map.106 = (bf16[512,4096]{1,0:T(8,128)(2,1)S(1)}, f32[256,512]{1,0:T(8,128)S(1)}, f32[8,128]{1,0:T(8,128)S(1)}) custom-call(bf16[512,4096]{1,0:T(8,128)(2,1)} %bitcast.2, bf16[4096,256]{1,0:T(8,128)(2,1)} %refs_1_.4, f32[8,128]{1,0:T(8,128)S(1)} %get-tuple-element.111.refs_2_), custom_call_target="tpu_custom_call" | custom-call | tf_op jit(solution)/shard_map/pallas_call | solution.py:59
  10.4 1.6 %collective-permute-start.2 = (f32[8,128]{1,0:T(8,128)S(1)}, f32[8,128]{1,0:T(8,128)S(1)}, u32[]{:S(2)}, u32[]{:S(2)}) collective-permute-start(f32[8,128]{1,0:T(8,128)S(1)} %get-tuple-element.119.refs_4_), channel_id=1, source_target_pairs={{0,4},{1,5},{2,6},{3,7},{4,0},{5,1},{6,2},{7,3},{8,12},{9,13},{10,... | collective-permute-start | bytes 12296 | tf_op jit(solution)/shard_map/ppermute | solution.py:28
  11.9 4.0 %shard_map.108 = (bf16[512,4096]{1,0:T(8,128)(2,1)S(1)}, f32[256,512]{1,0:T(8,128)S(1)}, f32[8,128]{1,0:T(8,128)S(1)}) custom-call(bf16[512,4096]{1,0:T(8,128)(2,1)} %bitcast.3, bf16[4096,256]{1,0:T(8,128)(2,1)} %refs_1_.5, f32[8,128]{1,0:T(8,128)S(1)} %get-tuple-element.116.refs_2_), custom_call_target="tpu_custom_call" | custom-call | tf_op jit(solution)/shard_map/pallas_call | solution.py:59
  16.0 0.2 shard_map.109
  16.2 0.5 shard_map.110
  16.8 0.5 shard_map.111
  17.2 0.5 collective-permute-start.5
  17.8 0.7 collective-permute-done.3.refs_4_
  18.5 0.5 shard_map.112
  18.9 0.7 shard_map.113
  19.8 0.5 shard_map.114
  20.3 0.5 shard_map.115
  20.7 0.4 collective-permute-start.7
  21.2 0.2 collective-permute-done.4.refs_4_
  21.4 0.7 shard_map.116
  22.2 0.5 shard_map.117
  22.8 0.5 shard_map.118
  23.3 1.2 %collective-permute-done.6.refs_4_ = f32[8,104,128]{2,1,0:T(8,128)S(1)} collective-permute-done((f32[8,104,128]{2,1,0:T(8,128)S(1)}, f32[8,104,128]{2,1,0:T(8,128)S(1)}, u32[]{:S(2)}, u32[]{:S(2)}) %collective-permute-start.6) | collective-permute-done | bytes 426016 | tf_op jit(solution)/shard_map/ppermute | solution.py:28
  24.5 0.5 shard_map.119
  24.9 2.0 %shard_map.120 = (f32[8,96,128]{2,1,0:T(8,128)S(1)}, f32[8,96,128]{2,1,0:T(8,128)S(1)}, f32[8,96,128]{2,1,0:T(8,128)S(1)}, f32[8,120,128]{2,1,0:T(8,128)S(1)}, f...) custom-call(bf16[512,4096]{1,0:T(8,128)(2,1)S(1)} %get-tuple-element.123.refs_0_, ...), custom_call_target="tpu_custom_call" | custom-call | tf_op jit(solution)/shard_map/pallas_call | solution.py:59
  27.1 0.4 collective-permute-start.11
  27.6 0.4 collective-permute-start.12
  28.2 0.6 collective-permute-done.8.refs_4_
  28.7 0.5 collective-permute-start.13
  29.2 0.7 collective-permute-done.9.refs_5_
  30.0 0.5 collective-permute-start.22
  30.5 0.7 collective-permute-done.10.refs_6_
  31.2 0.5 collective-permute-start.15
  31.7 1.6 %collective-permute-start.17 = (f32[8,96,128]{2,1,0:T(8,128)S(1)}, f32[8,96,128]{2,1,0:T(8,128)S(1)}, u32[]{:S(2)}, u32[]{:S(2)}) collective-permute-start(f32[8,96,128]{2,1,0:T(8,128)S(1)} %get-tuple-element.159), channel_id=1, source_target_pairs={{0,8},{1,9},{2,10},{3,11},{4,12},{5,13},{6,14},{7,15},{8,0},{9,1},... | collective-permute-start | bytes 1179656 | tf_op jit(solution)/shard_map/ppermute | solution.py:28
  33.3 1.1 %collective-permute-start.16 = (f32[8,96,128]{2,1,0:T(8,128)S(1)}, f32[8,96,128]{2,1,0:T(8,128)S(1)}, u32[]{:S(2)}, u32[]{:S(2)}) collective-permute-start(f32[8,96,128]{2,1,0:T(8,128)S(1)} %get-tuple-element.157), channel_id=1, source_target_pairs={{0,4},{1,5},{2,6},{3,7},{4,0},{5,1},{6,2},{7,3},{8,12},{9,13},{10,... | collective-permute-start | bytes 1179656 | tf_op jit(solution)/shard_map/ppermute | solution.py:28
  34.4 2.1 %shard_map.121 = (f32[8,96,128]{2,1,0:T(8,128)S(1)}, f32[8,96,128]{2,1,0:T(8,128)S(1)}, f32[8,96,128]{2,1,0:T(8,128)S(1)}, f32[8,120,128]{2,1,0:T(8,128)S(1)}, f...) custom-call(bf16[512,4096]{1,0:T(8,128)(2,1)S(1)} %get-tuple-element.123.refs_0_, ...), custom_call_target="tpu_custom_call" | custom-call | tf_op jit(solution)/shard_map/pallas_call | solution.py:59
  36.5 4.2 %collective-permute-done.13.refs_1_ = f32[8,96,128]{2,1,0:T(8,128)S(1)} collective-permute-done((f32[8,96,128]{2,1,0:T(8,128)S(1)}, f32[8,96,128]{2,1,0:T(8,128)S(1)}, u32[]{:S(2)}, u32[]{:S(2)}) %collective-permute-start.13) | collective-permute-done | bytes 393248 | tf_op jit(solution)/shard_map/ppermute | solution.py:28
  40.7 1.6 %collective-permute-start.14 = (f32[4,96,128]{2,1,0:T(8,128)S(1)}, f32[4,96,128]{2,1,0:T(8,128)S(1)}, u32[]{:S(2)}, u32[]{:S(2)}) collective-permute-start(f32[4,96,128]{2,1,0:T(8,128)S(1)} %get-tuple-element.153), channel_id=1, source_target_pairs={{0,8},{1,9},{2,10},{3,11},{4,12},{5,13},{6,14},{7,15},{8,0},{9,1},... | collective-permute-start | bytes 589832 | tf_op jit(solution)/shard_map/ppermute | solution.py:28
  42.4 0.9 collective-permute-done.17.refs_1_
  43.3 8.4 %collective-permute-done.16.refs_1_ = f32[8,96,128]{2,1,0:T(8,128)S(1)} collective-permute-done((f32[8,96,128]{2,1,0:T(8,128)S(1)}, f32[8,96,128]{2,1,0:T(8,128)S(1)}, u32[]{:S(2)}, u32[]{:S(2)}) %collective-permute-start.16) | collective-permute-done | bytes 393248 | tf_op jit(solution)/shard_map/ppermute | solution.py:28
  51.9 0.6 collective-permute-start.25
  52.5 0.5 collective-permute-start.20
  53.0 1.5 %collective-permute-start.21 = (f32[4,96,128]{2,1,0:T(8,128)S(1)}, f32[4,96,128]{2,1,0:T(8,128)S(1)}, u32[]{:S(2)}, u32[]{:S(2)}) collective-permute-start(f32[4,96,128]{2,1,0:T(8,128)S(1)} %get-tuple-element.171), channel_id=1, source_target_pairs={{0,2},{1,3},{2,0},{3,1},{4,6},{5,7},{6,4},{7,5},{8,10},{9,11},{10,... | collective-permute-start | bytes 589832 | tf_op jit(solution)/shard_map/ppermute | solution.py:28
  54.5 2.6 %collective-permute-start.19 = (f32[4,96,128]{2,1,0:T(8,128)S(1)}, f32[4,96,128]{2,1,0:T(8,128)S(1)}, u32[]{:S(2)}, u32[]{:S(2)}) collective-permute-start(f32[4,96,128]{2,1,0:T(8,128)S(1)} %get-tuple-element.167), channel_id=1, source_target_pairs={{0,16},{1,17},{2,18},{3,19},{4,20},{5,21},{6,22},{7,23},{8,24},{9,... | collective-permute-start | bytes 589832 | tf_op jit(solution)/shard_map/ppermute | solution.py:28
  57.1 0.3 collective-permute-start.18
  57.4 5.9 %collective-permute-done.21.refs_1_ = f32[4,96,128]{2,1,0:T(8,128)S(1)} collective-permute-done((f32[4,96,128]{2,1,0:T(8,128)S(1)}, f32[4,96,128]{2,1,0:T(8,128)S(1)}, u32[]{:S(2)}, u32[]{:S(2)}) %collective-permute-start.21) | collective-permute-done | bytes 196640 | tf_op jit(solution)/shard_map/ppermute | solution.py:28
  63.4 4.6 %collective-permute-done.19.refs_1_ = f32[4,96,128]{2,1,0:T(8,128)S(1)} collective-permute-done((f32[4,96,128]{2,1,0:T(8,128)S(1)}, f32[4,96,128]{2,1,0:T(8,128)S(1)}, u32[]{:S(2)}, u32[]{:S(2)}) %collective-permute-start.19) | collective-permute-done | bytes 196640 | tf_op jit(solution)/shard_map/ppermute | solution.py:28
  68.1 1.0 %collective-permute-done.18.refs_1_ = f32[2,96,128]{2,1,0:T(8,128)S(1)} collective-permute-done((f32[2,96,128]{2,1,0:T(8,128)S(1)}, f32[2,96,128]{2,1,0:T(8,128)S(1)}, u32[]{:S(2)}, u32[]{:S(2)}) %collective-permute-start.18) | collective-permute-done | bytes 98336 | tf_op jit(solution)/shard_map/ppermute | solution.py:28
  69.2 0.7 collective-permute-start.27
  69.9 1.4 %collective-permute-start.24 = (f32[2,104,128]{2,1,0:T(8,128)S(1)}, f32[2,104,128]{2,1,0:T(8,128)S(1)}, u32[]{:S(2)}, u32[]{:S(2)}) collective-permute-start(f32[2,104,128]{2,1,0:T(8,128)S(1)} %get-tuple-element.183), channel_id=1, source_target_pairs={{0,8},{1,9},{2,10},{3,11},{4,12},{5,13},{6,14},{7,15},{8,0},{9,1},... | collective-permute-start | bytes 319496 | tf_op jit(solution)/shard_map/ppermute | solution.py:28
  71.2 0.7 collective-permute-start.23
  71.9 1.5 %collective-permute-start.26 = (f32[2,96,128]{2,1,0:T(8,128)S(1)}, f32[2,96,128]{2,1,0:T(8,128)S(1)}, u32[]{:S(2)}, u32[]{:S(2)}) collective-permute-start(f32[2,96,128]{2,1,0:T(8,128)S(1)} %get-tuple-element.191), channel_id=1, source_target_pairs={{0,4},{1,5},{2,6},{3,7},{4,0},{5,1},{6,2},{7,3},{8,12},{9,13},{10,... | collective-permute-start | bytes 294920 | tf_op jit(solution)/shard_map/ppermute | solution.py:28
  73.4 3.4 %collective-permute-done.24.refs_1_ = f32[2,104,128]{2,1,0:T(8,128)S(1)} collective-permute-done((f32[2,104,128]{2,1,0:T(8,128)S(1)}, f32[2,104,128]{2,1,0:T(8,128)S(1)}, u32[]{:S(2)}, u32[]{:S(2)}) %collective-permute-start.24) | collective-permute-done | bytes 106528 | tf_op jit(solution)/shard_map/ppermute | solution.py:28
  76.9 1.0 %collective-permute-done.23.refs_1_ = f32[2,96,128]{2,1,0:T(8,128)S(1)} collective-permute-done((f32[2,96,128]{2,1,0:T(8,128)S(1)}, f32[2,96,128]{2,1,0:T(8,128)S(1)}, u32[]{:S(2)}, u32[]{:S(2)}) %collective-permute-start.23) | collective-permute-done | bytes 98336 | tf_op jit(solution)/shard_map/ppermute | solution.py:28
  78.0 3.3 %collective-permute-start.31 = (f32[1,120,128]{2,1,0:T(8,128)S(1)}, f32[1,120,128]{2,1,0:T(8,128)S(1)}, u32[]{:S(2)}, u32[]{:S(2)}) collective-permute-start(f32[1,120,128]{2,1,0:T(8,128)S(1)} %get-tuple-element.202), channel_id=1, source_target_pairs={{0,16},{1,17},{2,18},{3,19},{4,20},{5,21},{6,22},{7,23},{8,24},{9,... | collective-permute-start | bytes 184328 | tf_op jit(solution)/shard_map/ppermute | solution.py:28
  81.4 1.5 %collective-permute-start.28 = (f32[1,96,128]{2,1,0:T(8,128)S(1)}, f32[1,96,128]{2,1,0:T(8,128)S(1)}, u32[]{:S(2)}, u32[]{:S(2)}) collective-permute-start(f32[1,96,128]{2,1,0:T(8,128)S(1)} %get-tuple-element.199), channel_id=1, source_target_pairs={{0,4},{1,5},{2,6},{3,7},{4,0},{5,1},{6,2},{7,3},{8,12},{9,13},{10,... | collective-permute-start | bytes 147464 | tf_op jit(solution)/shard_map/ppermute | solution.py:28
  82.9 2.8 %collective-permute-start.29 = (f32[1,96,128]{2,1,0:T(8,128)S(1)}, f32[1,96,128]{2,1,0:T(8,128)S(1)}, u32[]{:S(2)}, u32[]{:S(2)}) collective-permute-start(f32[1,96,128]{2,1,0:T(8,128)S(1)} %get-tuple-element.200), channel_id=1, source_target_pairs={{0,16},{1,17},{2,18},{3,19},{4,20},{5,21},{6,22},{7,23},{8,24},{9,... | collective-permute-start | bytes 147464 | tf_op jit(solution)/shard_map/ppermute | solution.py:28
  85.7 0.4 collective-permute-start.30
  86.2 2.3 %collective-permute-done.29.refs_6_ = f32[1,96,128]{2,1,0:T(8,128)S(1)} collective-permute-done((f32[1,96,128]{2,1,0:T(8,128)S(1)}, f32[1,96,128]{2,1,0:T(8,128)S(1)}, u32[]{:S(2)}, u32[]{:S(2)}) %collective-permute-start.29) | collective-permute-done | bytes 49184 | tf_op jit(solution)/shard_map/ppermute | solution.py:28
  88.5 1.4 %collective-permute-done.30.refs_7_ = f32[1,96,128]{2,1,0:T(8,128)S(1)} collective-permute-done((f32[1,96,128]{2,1,0:T(8,128)S(1)}, f32[1,96,128]{2,1,0:T(8,128)S(1)}, u32[]{:S(2)}, u32[]{:S(2)}) %collective-permute-start.30) | collective-permute-done | bytes 49184 | tf_op jit(solution)/shard_map/ppermute | solution.py:28
  89.9 0.7 shard_map.137
  90.6 3.6 %all-to-all-start = ((f32[32,1,128]{2,1,0:T(1,128)}), f32[32,1,128]{2,1,0:T(1,128)S(1)}, u32[]{:S(2)}, u32[]{:S(2)}) async-start(f32[32,1,128]{2,1,0:T(1,128)} %get-tuple-element.207), calls=%async_computation | async-start | bytes 32768 | tf_op jit(solution)/shard_map/all_to_all | solution.py:324
  94.1 0.6 copy.11
  94.7 6.5 %all-to-all-done.refs_2_ = f32[32,1,128]{2,1,0:T(1,128)S(1)} async-done(((f32[32,1,128]{2,1,0:T(1,128)}), f32[32,1,128]{2,1,0:T(1,128)S(1)}, u32[]{:S(2)}, u32[]{:S(2)}) %all-to-all-start) | async-done | bytes 16416 | tf_op jit(solution)/shard_map/all_to_all | solution.py:324
  101.2 0.9 shard_map.138
  (48 shorter events, 1.8 us)
Async XLA Ops:
  1.3 0.7 copy-start.2
  2.1 1.3 %collective-permute-start = (f32[8,128]{1,0:T(8,128)S(1)}, f32[8,128]{1,0:T(8,128)S(1)}, u32[]{:S(2)}, u32[]{:S(2)}) collective-permute-start(f32[8,128]{1,0:T(8,128)S(1)} %get-tuple-element.107.refs_0_), channel_id=1, source_target_pairs={{0,1},{1,0},{2,3},{3,2},{4,5},{5,4},{6,7},{7,6},{8,9},{9,8},{10,11... | collective-permute-start | bytes 12296 | tf_op jit(solution)/shard_map/ppermute | solution.py:28
  3.4 6.9 %collective-permute-start.1 = (f32[8,128]{1,0:T(8,128)S(1)}, f32[8,128]{1,0:T(8,128)S(1)}, u32[]{:S(2)}, u32[]{:S(2)}) collective-permute-start(f32[8,128]{1,0:T(8,128)S(1)} %get-tuple-element.113.refs_0_), channel_id=1, source_target_pairs={{0,2},{1,3},{2,0},{3,1},{4,6},{5,7},{6,4},{7,5},{8,10},{9,11},{10,... | collective-permute-start | bytes 12296 | tf_op jit(solution)/shard_map/ppermute | solution.py:28
  10.3 5.7 %copy-start = (f32[1,512]{1,0:T(1,128)S(1)}, f32[1,512]{1,0:T(1,128)}, u32[]{:S(2)}) copy-start(f32[1,512]{1,0:T(1,128)} %refs_7_.1) | copy-start | bytes 6148
  10.3 5.7 %copy-start.1 = (f32[1,512]{1,0:T(1,128)S(1)}, f32[1,512]{1,0:T(1,128)}, u32[]{:S(2)}) copy-start(f32[1,512]{1,0:T(1,128)} %refs_8_.1) | copy-start | bytes 6148
  10.4 5.6 %collective-permute-start.2 = (f32[8,128]{1,0:T(8,128)S(1)}, f32[8,128]{1,0:T(8,128)S(1)}, u32[]{:S(2)}, u32[]{:S(2)}) collective-permute-start(f32[8,128]{1,0:T(8,128)S(1)} %get-tuple-element.119.refs_4_), channel_id=1, source_target_pairs={{0,4},{1,5},{2,6},{3,7},{4,0},{5,1},{6,2},{7,3},{8,12},{9,13},{10,... | collective-permute-start | bytes 12296 | tf_op jit(solution)/shard_map/ppermute | solution.py:28
  16.7 1.8 %collective-permute-start.3 = (f32[8,96,128]{2,1,0:T(8,128)S(1)}, f32[8,96,128]{2,1,0:T(8,128)S(1)}, u32[]{:S(2)}, u32[]{:S(2)}) collective-permute-start(f32[8,96,128]{2,1,0:T(8,128)S(1)} %get-tuple-element.128), channel_id=1, source_target_pairs={{0,1},{1,0},{2,3},{3,2},{4,5},{5,4},{6,7},{7,6},{8,9},{9,8},{10,11... | collective-permute-start | bytes 1179656 | tf_op jit(solution)/shard_map/ppermute | solution.py:28
  17.2 2.6 %collective-permute-start.5 = (f32[8,96,128]{2,1,0:T(8,128)S(1)}, f32[8,96,128]{2,1,0:T(8,128)S(1)}, u32[]{:S(2)}, u32[]{:S(2)}) collective-permute-start(f32[8,96,128]{2,1,0:T(8,128)S(1)} %get-tuple-element.133), channel_id=1, source_target_pairs={{0,1},{1,0},{2,3},{3,2},{4,5},{5,4},{6,7},{7,6},{8,9},{9,8},{10,11... | collective-permute-start | bytes 1179656 | tf_op jit(solution)/shard_map/ppermute | solution.py:28
  19.7 1.7 %collective-permute-start.4 = (f32[8,96,128]{2,1,0:T(8,128)S(1)}, f32[8,96,128]{2,1,0:T(8,128)S(1)}, u32[]{:S(2)}, u32[]{:S(2)}) collective-permute-start(f32[8,96,128]{2,1,0:T(8,128)S(1)} %get-tuple-element.132), channel_id=1, source_target_pairs={{0,1},{1,0},{2,3},{3,2},{4,5},{5,4},{6,7},{7,6},{8,9},{9,8},{10,11... | collective-permute-start | bytes 1179656 | tf_op jit(solution)/shard_map/ppermute | solution.py:28
  20.7 2.1 %collective-permute-start.7 = (f32[8,120,128]{2,1,0:T(8,128)S(1)}, f32[8,120,128]{2,1,0:T(8,128)S(1)}, u32[]{:S(2)}, u32[]{:S(2)}) collective-permute-start(f32[8,120,128]{2,1,0:T(8,128)S(1)} %get-tuple-element.139), channel_id=1, source_target_pairs={{0,1},{1,0},{2,3},{3,2},{4,5},{5,4},{6,7},{7,6},{8,9},{9,8},{10,11... | collective-permute-start | bytes 1474568 | tf_op jit(solution)/shard_map/ppermute | solution.py:28
  22.6 1.8 %collective-permute-start.6 = (f32[8,104,128]{2,1,0:T(8,128)S(1)}, f32[8,104,128]{2,1,0:T(8,128)S(1)}, u32[]{:S(2)}, u32[]{:S(2)}) collective-permute-start(f32[8,104,128]{2,1,0:T(8,128)S(1)} %get-tuple-element.138), channel_id=1, source_target_pairs={{0,1},{1,0},{2,3},{3,2},{4,5},{5,4},{6,7},{7,6},{8,9},{9,8},{10,11... | collective-permute-start | bytes 1277960 | tf_op jit(solution)/shard_map/ppermute | solution.py:28
  26.9 1.8 %collective-permute-start.8 = (f32[8,96,128]{2,1,0:T(8,128)S(1)}, f32[8,96,128]{2,1,0:T(8,128)S(1)}, u32[]{:S(2)}, u32[]{:S(2)}) collective-permute-start(f32[8,96,128]{2,1,0:T(8,128)S(1)} %get-tuple-element.143), channel_id=1, source_target_pairs={{0,1},{1,0},{2,3},{3,2},{4,5},{5,4},{6,7},{7,6},{8,9},{9,8},{10,11... | collective-permute-start | bytes 1179656 | tf_op jit(solution)/shard_map/ppermute | solution.py:28
  27.1 6.1 %collective-permute-start.11 = (f32[8,120,128]{2,1,0:T(8,128)S(1)}, f32[8,120,128]{2,1,0:T(8,128)S(1)}, u32[]{:S(2)}, u32[]{:S(2)}) collective-permute-start(f32[8,120,128]{2,1,0:T(8,128)S(1)} %get-tuple-element.146), channel_id=1, source_target_pairs={{0,1},{1,0},{2,3},{3,2},{4,5},{5,4},{6,7},{7,6},{8,9},{9,8},{10,11... | collective-permute-start | bytes 1474568 | tf_op jit(solution)/shard_map/ppermute | solution.py:28
  27.5 2.5 %collective-permute-start.9 = (f32[8,96,128]{2,1,0:T(8,128)S(1)}, f32[8,96,128]{2,1,0:T(8,128)S(1)}, u32[]{:S(2)}, u32[]{:S(2)}) collective-permute-start(f32[8,96,128]{2,1,0:T(8,128)S(1)} %get-tuple-element.144), channel_id=1, source_target_pairs={{0,1},{1,0},{2,3},{3,2},{4,5},{5,4},{6,7},{7,6},{8,9},{9,8},{10,11... | collective-permute-start | bytes 1179656 | tf_op jit(solution)/shard_map/ppermute | solution.py:28
  27.6 4.0 %collective-permute-start.12 = (f32[8,104,128]{2,1,0:T(8,128)S(1)}, f32[8,104,128]{2,1,0:T(8,128)S(1)}, u32[]{:S(2)}, u32[]{:S(2)}) collective-permute-start(f32[8,104,128]{2,1,0:T(8,128)S(1)} %get-tuple-element.147), channel_id=1, source_target_pairs={{0,1},{1,0},{2,3},{3,2},{4,5},{5,4},{6,7},{7,6},{8,9},{9,8},{10,11... | collective-permute-start | bytes 1277960 | tf_op jit(solution)/shard_map/ppermute | solution.py:28
  28.0 3.1 %collective-permute-start.10 = (f32[8,96,128]{2,1,0:T(8,128)S(1)}, f32[8,96,128]{2,1,0:T(8,128)S(1)}, u32[]{:S(2)}, u32[]{:S(2)}) collective-permute-start(f32[8,96,128]{2,1,0:T(8,128)S(1)} %get-tuple-element.145), channel_id=1, source_target_pairs={{0,1},{1,0},{2,3},{3,2},{4,5},{5,4},{6,7},{7,6},{8,9},{9,8},{10,11... | collective-permute-start | bytes 1179656 | tf_op jit(solution)/shard_map/ppermute | solution.py:28
  28.7 12.0 %collective-permute-start.13 = (f32[8,96,128]{2,1,0:T(8,128)S(1)}, f32[8,96,128]{2,1,0:T(8,128)S(1)}, u32[]{:S(2)}, u32[]{:S(2)}) collective-permute-start(f32[8,96,128]{2,1,0:T(8,128)S(1)} %get-tuple-element.150), channel_id=1, source_target_pairs={{0,2},{1,3},{2,0},{3,1},{4,6},{5,7},{6,4},{7,5},{8,10},{9,11},{10,... | collective-permute-start | bytes 1179656 | tf_op jit(solution)/shard_map/ppermute | solution.py:28
  30.0 21.9 %collective-permute-start.22 = (f32[8,120,128]{2,1,0:T(8,128)S(1)}, f32[8,120,128]{2,1,0:T(8,128)S(1)}, u32[]{:S(2)}, u32[]{:S(2)}) collective-permute-start(f32[8,120,128]{2,1,0:T(8,128)S(1)} %get-tuple-element.173), channel_id=1, source_target_pairs={{0,4},{1,5},{2,6},{3,7},{4,0},{5,1},{6,2},{7,3},{8,12},{9,13},{10,... | collective-permute-start | bytes 1474568 | tf_op jit(solution)/shard_map/ppermute | solution.py:28
  31.2 20.6 %collective-permute-start.15 = (f32[8,104,128]{2,1,0:T(8,128)S(1)}, f32[8,104,128]{2,1,0:T(8,128)S(1)}, u32[]{:S(2)}, u32[]{:S(2)}) collective-permute-start(f32[8,104,128]{2,1,0:T(8,128)S(1)} %get-tuple-element.155), channel_id=1, source_target_pairs={{0,2},{1,3},{2,0},{3,1},{4,6},{5,7},{6,4},{7,5},{8,10},{9,11},{10,... | collective-permute-start | bytes 1277960 | tf_op jit(solution)/shard_map/ppermute | solution.py:28
  31.7 11.6 %collective-permute-start.17 = (f32[8,96,128]{2,1,0:T(8,128)S(1)}, f32[8,96,128]{2,1,0:T(8,128)S(1)}, u32[]{:S(2)}, u32[]{:S(2)}) collective-permute-start(f32[8,96,128]{2,1,0:T(8,128)S(1)} %get-tuple-element.159), channel_id=1, source_target_pairs={{0,8},{1,9},{2,10},{3,11},{4,12},{5,13},{6,14},{7,15},{8,0},{9,1},... | collective-permute-start | bytes 1179656 | tf_op jit(solution)/shard_map/ppermute | solution.py:28
  33.3 18.4 %collective-permute-start.16 = (f32[8,96,128]{2,1,0:T(8,128)S(1)}, f32[8,96,128]{2,1,0:T(8,128)S(1)}, u32[]{:S(2)}, u32[]{:S(2)}) collective-permute-start(f32[8,96,128]{2,1,0:T(8,128)S(1)} %get-tuple-element.157), channel_id=1, source_target_pairs={{0,4},{1,5},{2,6},{3,7},{4,0},{5,1},{6,2},{7,3},{8,12},{9,13},{10,... | collective-permute-start | bytes 1179656 | tf_op jit(solution)/shard_map/ppermute | solution.py:28
  40.7 11.0 %collective-permute-start.14 = (f32[4,96,128]{2,1,0:T(8,128)S(1)}, f32[4,96,128]{2,1,0:T(8,128)S(1)}, u32[]{:S(2)}, u32[]{:S(2)}) collective-permute-start(f32[4,96,128]{2,1,0:T(8,128)S(1)} %get-tuple-element.153), channel_id=1, source_target_pairs={{0,8},{1,9},{2,10},{3,11},{4,12},{5,13},{6,14},{7,15},{8,0},{9,1},... | collective-permute-start | bytes 589832 | tf_op jit(solution)/shard_map/ppermute | solution.py:28
  51.9 17.2 %collective-permute-start.25 = (f32[4,120,128]{2,1,0:T(8,128)S(1)}, f32[4,120,128]{2,1,0:T(8,128)S(1)}, u32[]{:S(2)}, u32[]{:S(2)}) collective-permute-start(f32[4,120,128]{2,1,0:T(8,128)S(1)} %get-tuple-element.185), channel_id=1, source_target_pairs={{0,2},{1,3},{2,0},{3,1},{4,6},{5,7},{6,4},{7,5},{8,10},{9,11},{10,... | collective-permute-start | bytes 737288 | tf_op jit(solution)/shard_map/ppermute | solution.py:28
  52.5 10.9 %collective-permute-start.20 = (f32[4,104,128]{2,1,0:T(8,128)S(1)}, f32[4,104,128]{2,1,0:T(8,128)S(1)}, u32[]{:S(2)}, u32[]{:S(2)}) collective-permute-start(f32[4,104,128]{2,1,0:T(8,128)S(1)} %get-tuple-element.169), channel_id=1, source_target_pairs={{0,4},{1,5},{2,6},{3,7},{4,0},{5,1},{6,2},{7,3},{8,12},{9,13},{10,... | collective-permute-start | bytes 638984 | tf_op jit(solution)/shard_map/ppermute | solution.py:28
  53.0 10.4 %collective-permute-start.21 = (f32[4,96,128]{2,1,0:T(8,128)S(1)}, f32[4,96,128]{2,1,0:T(8,128)S(1)}, u32[]{:S(2)}, u32[]{:S(2)}) collective-permute-start(f32[4,96,128]{2,1,0:T(8,128)S(1)} %get-tuple-element.171), channel_id=1, source_target_pairs={{0,2},{1,3},{2,0},{3,1},{4,6},{5,7},{6,4},{7,5},{8,10},{9,11},{10,... | collective-permute-start | bytes 589832 | tf_op jit(solution)/shard_map/ppermute | solution.py:28
  54.5 13.5 %collective-permute-start.19 = (f32[4,96,128]{2,1,0:T(8,128)S(1)}, f32[4,96,128]{2,1,0:T(8,128)S(1)}, u32[]{:S(2)}, u32[]{:S(2)}) collective-permute-start(f32[4,96,128]{2,1,0:T(8,128)S(1)} %get-tuple-element.167), channel_id=1, source_target_pairs={{0,16},{1,17},{2,18},{3,19},{4,20},{5,21},{6,22},{7,23},{8,24},{9,... | collective-permute-start | bytes 589832 | tf_op jit(solution)/shard_map/ppermute | solution.py:28
  57.1 12.0 %collective-permute-start.18 = (f32[2,96,128]{2,1,0:T(8,128)S(1)}, f32[2,96,128]{2,1,0:T(8,128)S(1)}, u32[]{:S(2)}, u32[]{:S(2)}) collective-permute-start(f32[2,96,128]{2,1,0:T(8,128)S(1)} %get-tuple-element.165), channel_id=1, source_target_pairs={{0,16},{1,17},{2,18},{3,19},{4,20},{5,21},{6,22},{7,23},{8,24},{9,... | collective-permute-start | bytes 294920 | tf_op jit(solution)/shard_map/ppermute | solution.py:28
  69.2 8.8 %collective-permute-start.27 = (f32[2,120,128]{2,1,0:T(8,128)S(1)}, f32[2,120,128]{2,1,0:T(8,128)S(1)}, u32[]{:S(2)}, u32[]{:S(2)}) collective-permute-start(f32[2,120,128]{2,1,0:T(8,128)S(1)} %get-tuple-element.193), channel_id=1, source_target_pairs={{0,8},{1,9},{2,10},{3,11},{4,12},{5,13},{6,14},{7,15},{8,0},{9,1},... | collective-permute-start | bytes 368648 | tf_op jit(solution)/shard_map/ppermute | solution.py:28
  69.9 7.0 %collective-permute-start.24 = (f32[2,104,128]{2,1,0:T(8,128)S(1)}, f32[2,104,128]{2,1,0:T(8,128)S(1)}, u32[]{:S(2)}, u32[]{:S(2)}) collective-permute-start(f32[2,104,128]{2,1,0:T(8,128)S(1)} %get-tuple-element.183), channel_id=1, source_target_pairs={{0,8},{1,9},{2,10},{3,11},{4,12},{5,13},{6,14},{7,15},{8,0},{9,1},... | collective-permute-start | bytes 319496 | tf_op jit(solution)/shard_map/ppermute | solution.py:28
  71.2 6.7 %collective-permute-start.23 = (f32[2,96,128]{2,1,0:T(8,128)S(1)}, f32[2,96,128]{2,1,0:T(8,128)S(1)}, u32[]{:S(2)}, u32[]{:S(2)}) collective-permute-start(f32[2,96,128]{2,1,0:T(8,128)S(1)} %get-tuple-element.181), channel_id=1, source_target_pairs={{0,8},{1,9},{2,10},{3,11},{4,12},{5,13},{6,14},{7,15},{8,0},{9,1},... | collective-permute-start | bytes 294920 | tf_op jit(solution)/shard_map/ppermute | solution.py:28
  71.9 13.8 %collective-permute-start.26 = (f32[2,96,128]{2,1,0:T(8,128)S(1)}, f32[2,96,128]{2,1,0:T(8,128)S(1)}, u32[]{:S(2)}, u32[]{:S(2)}) collective-permute-start(f32[2,96,128]{2,1,0:T(8,128)S(1)} %get-tuple-element.191), channel_id=1, source_target_pairs={{0,4},{1,5},{2,6},{3,7},{4,0},{5,1},{6,2},{7,3},{8,12},{9,13},{10,... | collective-permute-start | bytes 294920 | tf_op jit(solution)/shard_map/ppermute | solution.py:28
  78.0 11.9 %collective-permute-start.31 = (f32[1,120,128]{2,1,0:T(8,128)S(1)}, f32[1,120,128]{2,1,0:T(8,128)S(1)}, u32[]{:S(2)}, u32[]{:S(2)}) collective-permute-start(f32[1,120,128]{2,1,0:T(8,128)S(1)} %get-tuple-element.202), channel_id=1, source_target_pairs={{0,16},{1,17},{2,18},{3,19},{4,20},{5,21},{6,22},{7,23},{8,24},{9,... | collective-permute-start | bytes 184328 | tf_op jit(solution)/shard_map/ppermute | solution.py:28
  81.3 7.2 %collective-permute-start.32 = (f32[1,104,128]{2,1,0:T(8,128)S(1)}, f32[1,104,128]{2,1,0:T(8,128)S(1)}, u32[]{:S(2)}, u32[]{:S(2)}) collective-permute-start(f32[1,104,128]{2,1,0:T(8,128)S(1)} %get-tuple-element.203), channel_id=1, source_target_pairs={{0,16},{1,17},{2,18},{3,19},{4,20},{5,21},{6,22},{7,23},{8,24},{9,... | collective-permute-start | bytes 159752 | tf_op jit(solution)/shard_map/ppermute | solution.py:28
  81.4 4.8 %collective-permute-start.28 = (f32[1,96,128]{2,1,0:T(8,128)S(1)}, f32[1,96,128]{2,1,0:T(8,128)S(1)}, u32[]{:S(2)}, u32[]{:S(2)}) collective-permute-start(f32[1,96,128]{2,1,0:T(8,128)S(1)} %get-tuple-element.199), channel_id=1, source_target_pairs={{0,4},{1,5},{2,6},{3,7},{4,0},{5,1},{6,2},{7,3},{8,12},{9,13},{10,... | collective-permute-start | bytes 147464 | tf_op jit(solution)/shard_map/ppermute | solution.py:28
  82.9 5.6 %collective-permute-start.29 = (f32[1,96,128]{2,1,0:T(8,128)S(1)}, f32[1,96,128]{2,1,0:T(8,128)S(1)}, u32[]{:S(2)}, u32[]{:S(2)}) collective-permute-start(f32[1,96,128]{2,1,0:T(8,128)S(1)} %get-tuple-element.200), channel_id=1, source_target_pairs={{0,16},{1,17},{2,18},{3,19},{4,20},{5,21},{6,22},{7,23},{8,24},{9,... | collective-permute-start | bytes 147464 | tf_op jit(solution)/shard_map/ppermute | solution.py:28
  85.7 4.2 %collective-permute-start.30 = (f32[1,96,128]{2,1,0:T(8,128)S(1)}, f32[1,96,128]{2,1,0:T(8,128)S(1)}, u32[]{:S(2)}, u32[]{:S(2)}) collective-permute-start(f32[1,96,128]{2,1,0:T(8,128)S(1)} %get-tuple-element.201), channel_id=1, source_target_pairs={{0,2},{1,3},{2,0},{3,1},{4,6},{5,7},{6,4},{7,5},{8,10},{9,11},{10,... | collective-permute-start | bytes 147464 | tf_op jit(solution)/shard_map/ppermute | solution.py:28
  90.6 10.7 %all-to-all-start = ((f32[32,1,128]{2,1,0:T(1,128)}), f32[32,1,128]{2,1,0:T(1,128)S(1)}, u32[]{:S(2)}, u32[]{:S(2)}) async-start(f32[32,1,128]{2,1,0:T(1,128)} %get-tuple-element.207), calls=%async_computation | async-start | bytes 32768 | tf_op jit(solution)/shard_map/all_to_all | solution.py:324
where the time goes:
time: 102 us
  waiting for transfers between devices  44.5 us (44%)
  starting transfers between devices  35 us (34%)
  Pallas kernels  19.9 us (20%)
  between operations  1.54 us (2%)
  local copies, waits for them, and re-layouts  1.27 us (1%)
    ppermute x33, waiting for transfers between devices, swap(): return lax.ppermute(x, AXES, [(i, i ^ mask) for i in range(count)])  37.9 us
    ppermute x33, starting transfers between devices, swap(): return lax.ppermute(x, AXES, [(i, i ^ mask) for i in range(count)])  31.4 us
    pallas_call x36, Pallas kernels, call(): *got, self.token = kernel(*scalars, *from_hbm, *ins)  19.9 us
    all_to_all x1, waiting for transfers between devices, in_blocks(): squares = lax.all_to_all(squares, AXES, 0, 0, tiled=True)  6.52 us
    all_to_all x1, starting transfers between devices, in_blocks(): squares = lax.all_to_all(squares, AXES, 0, 0, tiled=True)  3.56 us
  transfers between devices with their start and end apart: 34, of which 18 were waited for; matrix products, arithmetic and copies ran while one was open for 1% of the time, Pallas kernels for 15%

commit v1 on v0

--- a/solution.py
+++ b/solution.py
@@ -16,8 +16,8 @@
 KERNEL_VMEM = 8 * 1024 * 1024
 F32 = jnp.float32
 
-PARTS = (("xzy", 12), ("yxz", 12), ("zyx", 12), ("yxz", 15), ("xyz", 13))
-TURNS = (0, 2, 1, 4, 0, 3, 1, 4, 2, 0, 3, 4, 1, 3, 2)
+PARTS = (("zxyw", 19), ("yxzw", 17), ("xyzw", 16), ("wyzx", 12))
+TURNS = (1, 2, 0, 2, 3, 1, 2, 0, 3, 1, 0, 3)
 
 SMEM = pl.BlockSpec(memory_space=pltpu.SMEM)
 VMEM = pl.BlockSpec(memory_space=pltpu.VMEM)
@@ -31,8 +31,14 @@
 class Line:
     def __init__(self):
         self.token = None
-
-    def call(self, body, outs, ins, scalars=(), from_hbm=(), scratch=(), in_vmem=True):
+        self.placed = {}
+
+    def place(self, x):
+        x = pltpu.with_memory_space_constraint(x, pltpu.VMEM)
+        self.placed[id(x)] = x
+        return x
+
+    def call(self, body, outs, ins, scalars=(), from_hbm=(), scratch=(), in_vmem=True, flops=0):
         first = self.token is None
         n_in = len(scalars) + len(from_hbm) + len(ins)
 
@@ -53,9 +59,10 @@
             out_specs=(VMEM,) * (len(outs) + 1),
             scratch_shapes=list(scratch),
             compiler_params=pltpu.CompilerParams(vmem_limit_bytes=KERNEL_VMEM),
+            cost_estimate=pl.CostEstimate(flops=flops, bytes_accessed=0, transcendentals=0) if flops else None,
         )
         from_hbm = [pltpu.with_memory_space_constraint(x, pltpu.HBM) for x in from_hbm]
-        ins = [pltpu.with_memory_space_constraint(x, pltpu.VMEM) for x in [*ins, *tokens]]
+        ins = [x if id(x) in self.placed else pltpu.with_memory_space_constraint(x, pltpu.VMEM) for x in [*ins, *tokens]]
         *got, self.token = kernel(*scalars, *from_hbm, *ins)
         return got
 
@@ -86,19 +93,9 @@
     new_group[...], new_carried[...] = carry(group[...], other[...], carried[...], **sizes)
 
 
-def project_body(src_hbm, mat_hbm, src, out_t, mat, acc, src_sems, mat_sems, *, steps):
-    width = src.shape[1]
-    step = width // steps
-    copies = []
+def project_body(src, mat, out_t, acc, *, steps):
+    step = src.shape[1] // steps
     for i in range(steps):
-        cut = pl.ds(i * step, step)
-        copies.append(pltpu.make_async_copy(src_hbm.at[:, cut], src.at[:, cut], src_sems.at[i]))
-        copies.append(pltpu.make_async_copy(mat_hbm.at[cut, :], mat.at[cut, :], mat_sems.at[i]))
-    for c in copies:
-        c.start()
-    for i in range(steps):
-        copies[2 * i].wait()
-        copies[2 * i + 1].wait()
         cut = slice(i * step, (i + 1) * step)
         part = jnp.dot(src[:, cut], mat[cut, :], preferred_element_type=F32)
         if i:
@@ -148,10 +145,8 @@
     scaled_down[...] = (weight * down_t[...]).astype(jnp.bfloat16)
 
 
-def blocks_body(*refs, jobs, seq_size, n_out, adds):
-    hid, direction, scaled_up, scaled_down = refs[:4]
-    received = refs[4 : 4 + n_out] if adds else ()
-    outs = refs[4 + n_out :] if adds else refs[4:]
+def blocks_body(*refs, jobs, seq_size):
+    hid, direction, scaled_up, scaled_down, *outs = refs
     me = lax.axis_index("batch") * seq_size + lax.axis_index("seq")
     for out_at, tiles, row_at, rows, side, from_row in jobs:
         src, weight = ((hid, scaled_up), (direction, scaled_down))[side]
@@ -162,13 +157,10 @@
             block = jnp.concatenate(cols, axis=1) if len(cols) > 1 else cols[0]
             grad = jnp.dot(weight[from_row : from_row + rows, :], block, preferred_element_type=F32)
             for j in range(len(pair)):
-                part = grad[:, j * LANES : (j + 1) * LANES]
-                if adds:
-                    part = part + received[out_at][i + j, row_at : row_at + rows, :]
-                out[i + j, row_at : row_at + rows, :] = part
-
-
-def blocks(line, ops, wanted, received, seq_size):
+                out[i + j, row_at : row_at + rows, :] = grad[:, j * LANES : (j + 1) * LANES]
+
+
+def blocks(line, ops, wanted, seq_size):
     jobs, shapes = [], []
     for out_at, (tiles, pieces) in enumerate(wanted):
         at = 0
@@ -176,17 +168,18 @@
             jobs.append((out_at, tuple(tiles), at, rows, side, from_row))
             at += rows
         shapes.append(((len(tiles), at, LANES), F32))
-    extra = tuple(received) if received is not None else ()
-    body = functools.partial(
-        blocks_body, jobs=tuple(jobs), seq_size=seq_size, n_out=len(wanted), adds=received is not None
-    )
-    return line.call(body, shapes, (*ops, *extra))
-
-
-def fold_body(keep, got, send, left):
+    return line.call(functools.partial(blocks_body, jobs=tuple(jobs), seq_size=seq_size), shapes, ops)
+
+
+def add_body(a, b, out):
+    out[...] = a[...] + b[...]
+
+
+def fold_body(*refs):
+    *terms, send, left = refs
     half = send.shape[0]
-    send[...] = keep[half:] + got[half:]
-    left[...] = keep[:half] + got[:half]
+    send[...] = functools.reduce(jnp.add, [t[half:] for t in terms])
+    left[...] = functools.reduce(jnp.add, [t[:half] for t in terms])
 
 
 def total_body(*refs, n, rank):
@@ -223,9 +216,19 @@
     return n.bit_length() - 1
 
 
-def turns_of(halvings):
+def script(halvings):
     n = len(PARTS)
-    return TURNS if len(TURNS) == n * (halvings - 1) else [i for _ in range(halvings - 1) for i in range(n)]
+    first = list(range(n))
+    steps = [("blocks", 0, 0)]
+    for i in first:
+        steps += [("blocks", i + 1, 0), ("add", i, 0)]
+    steps += [("far_rest", 0, 0), ("near_rest", 0, 0)]
+    turns = TURNS if len(TURNS) == n * (halvings - 1) else first * (halvings - 1)
+    taken = [1] * n
+    for i in turns:
+        steps.append(("fold", i, taken[i]))
+        taken[i] += 1
+    return steps
 
 
 def local_blocks(hidden, score_direction, adapter_down, adapter_up, rewards, values, log_ratio, lengths):
@@ -243,39 +246,32 @@
 
     bits = [1 << j for j in range(log2(ns))]
     tile = ((8, LANES), F32)
+    FL = 40_000_000_000
     live, group = line.call(
         functools.partial(first_body, total_len=total_len), [((1, tokens), F32), tile], (rewards,), (lengths,)
     )
     carried = jnp.zeros(*tile)
-    steps = 8
-    under = [(hid_hbm, adapter_down), (direction_hbm, adapter_up)]
+    hid, direction = line.place(hid_hbm), line.place(direction_hbm)
+    under = [(hid, adapter_down), (direction, adapter_up)]
     made = []
     for j, side in enumerate(bits):
         other = swap(group, side, count)
         if j == 0:
-            (within,) = line.call(functools.partial(within_body, total_len=total_len), [((1, tokens), F32)], (live,))
+            (within,) = line.call(functools.partial(within_body, total_len=total_len), [((1, tokens), F32)], (live,), flops=FL)
         if j >= len(bits) - len(under):
-            src, mat = under[len(made)]
-            made.append(
-                line.call(
-                    functools.partial(project_body, steps=steps),
-                    [((tokens, width), src.dtype), ((rank, tokens), F32)],
-                    (),
-                    from_hbm=(src, mat),
-                    scratch=[
-                        pltpu.VMEM((width, rank), mat.dtype),
-                        pltpu.VMEM((tokens, rank), F32),
-                        pltpu.SemaphoreType.DMA((steps,)),
-                        pltpu.SemaphoreType.DMA((steps,)),
-                    ],
-                )
+            (proj,) = line.call(
+                functools.partial(project_body, steps=2),
+                [((rank, tokens), F32)],
+                under[len(made)],
+                scratch=[pltpu.VMEM((tokens, rank), F32)],
             )
+            made.append(proj)
         if j < len(bits) - 1:
             group, carried = line.call(
                 functools.partial(carry_body, side=side, tokens=tokens, total_len=total_len),
                 [tile, tile], (group, other, carried),
             )
-    (hid, down_t), (direction, up_t) = made
+    down_t, up_t = made
     returns, scaled_up, scaled_down = line.call(
         functools.partial(weigh_body, side=bits[-1], total_len=total_len, seq_total=nb),
         [((1, tokens), F32), ((rank, tokens), jnp.bfloat16), ((rank, tokens), jnp.bfloat16)],
@@ -284,7 +280,8 @@
 
     ops = (hid, direction, scaled_up, scaled_down)
     core, plane = bits[0], bits[1:]
-    masks = {"x": plane[: len(plane) // 2], "y": plane[len(plane) // 2 :], "z": [ns << j for j in range(log2(nb))]}
+    zs = [ns << j for j in range(log2(nb))]
+    masks = {"x": plane[: len(plane) // 2], "y": plane[len(plane) // 2 :], "z": zs[:-1], "w": zs[-1:]}
     orders, pieces, at = [], [], 0
     for axes, share in PARTS:
         orders.append([m for axis in axes for m in masks[axis]])
@@ -299,27 +296,32 @@
     sends = [(tiles_of(orders[i][1:], orders[i][0]), pieces[i]) for i in range(n)]
     stays = [(tiles_of(orders[i][1:], 0), pieces[i]) for i in range(n)]
     far = lambda w: ([t | core for t in w[0]], w[1])
-    got, sent, theirs = [None] * n, [None] * n, [None] * n
-    for i in range(n + 1):
-        if i < n:
-            (theirs[i],) = blocks(line, ops, [far(sends[i])], None, ns)
-            got[i] = swap(theirs[i], core, count)
-        if i:
-            (mine,) = blocks(line, ops, [sends[i - 1]], [got[i - 1]], ns)
-            sent[i - 1] = swap(mine, orders[i - 1][0], count)
-    got = [swap(t, core, count) for t in blocks(line, ops, [far(w) for w in stays], None, ns)]
-    kept = blocks(line, ops, stays, got, ns)
-
-    taken = [1] * n
-    for i in turns_of(len(orders[0])):
-        blocks_now, rows, _ = kept[i].shape
-        send, kept[i] = line.call(fold_body, [((blocks_now // 2, rows, LANES), F32)] * 2, (kept[i], sent[i]))
-        sent[i] = swap(send, orders[i][taken[i]], count)
-        taken[i] += 1
+    got, near, sent, kept = [None] * n, [None] * n, [None] * n, [None] * n
+    for name, i, k in script(len(orders[0])):
+        if name == "blocks":
+            want = ([sends[i - 1]] if i else []) + ([far(sends[i])] if i < n else [])
+            made = list(blocks(line, ops, want, ns))
+            if i:
+                near[i - 1] = made.pop(0)
+            if i < n:
+                got[i] = swap(made[0], core, count)
+        elif name == "far_rest":
+            rest = [swap(t, core, count) for t in blocks(line, ops, [far(w) for w in stays], ns)]
+        elif name == "near_rest":
+            kept = [(a, b) for a, b in zip(blocks(line, ops, stays, ns), rest)]
+        else:
+            if name == "add":
+                (send,) = line.call(add_body, [(near[i].shape, F32)], (near[i], got[i]))
+            else:
+                terms = (*kept[i], sent[i])
+                blocks_now, rows, _ = terms[0].shape
+                send, left = line.call(fold_body, [((blocks_now // 2, rows, LANES), F32)] * 2, terms)
+                kept[i] = (left,)
+            sent[i] = swap(send, orders[i][k], count)
 
     down, up, squares = line.call(
         functools.partial(total_body, n=n, rank=rank),
-        [((rank, LANES), F32), ((rank, LANES), F32), ((count, 1, LANES), F32)], (*kept, *sent),
+        [((rank, LANES), F32), ((rank, LANES), F32), ((count, 1, LANES), F32)], (*[k[0] for k in kept], *sent),
     )
     squares = lax.all_to_all(squares, AXES, 0, 0, tiled=True)
     clip_norm = 0.5 * math.sqrt(2.0 * width * rank)

time: 102 us -> 91.6 us (0.90)
  Pallas kernels: 19.9 us -> 12.9 us
  waiting for transfers between devices: 44.5 us -> 41.9 us
  starting transfers between devices: 35 us -> 33.9 us
    pallas_call x36 -> x32, Pallas kernels: 19.9 us -> 12.9 us  [call(): *got, self.token = kernel(*scalars, *from_hbm, *ins)]
    ppermute x33 -> x27, waiting for transfers between devices: 37.9 us -> 35.3 us  [swap(): return lax.ppermute(x, AXES, [(i, i ^ mask) for i in range(count)])]
    ppermute x33 -> x27, starting transfers between devices: 31.4 us -> 29.7 us  [swap(): return lax.ppermute(x, AXES, [(i, i ^ mask) for i in range(count)])]
  transfers between devices with their start and end apart: 34 -> 28, of which waited for: 18 -> 15; matrix products, arithmetic and copies ran while one was open for 1% -> 1% of each run, Pallas kernels for 15% -> 12%
where the time goes in v1:
time: 91.6 us; the launch traced here: 91.4 us
  waiting for transfers between devices  41.9 us (46%)
  starting transfers between devices  33.9 us (37%)
  Pallas kernels  12.9 us (14%)
  between operations  1.48 us (2%)
  local copies, waits for them, and re-layouts  1.29 us (1%)
    ppermute x27, waiting for transfers between devices, swap(): return lax.ppermute(x, AXES, [(i, i ^ mask) for i in range(count)])  35.3 us
    ppermute x27, starting transfers between devices, swap(): return lax.ppermute(x, AXES, [(i, i ^ mask) for i in range(count)])  29.7 us
    pallas_call x32, Pallas kernels, call(): *got, self.token = kernel(*scalars, *from_hbm, *ins)  12.9 us
    all_to_all x1, waiting for transfers between devices, in_blocks(): squares = lax.all_to_all(squares, AXES, 0, 0, tiled=True)  6.52 us
    all_to_all x1, starting transfers between devices, in_blocks(): squares = lax.all_to_all(squares, AXES, 0, 0, tiled=True)  4.19 us
  transfers between devices with their start and end apart: 28, of which 15 were waited for; matrix products, arithmetic and copies ran while one was open for 1% of the time, Pallas kernels for 12%

profile of v1, /device:TPU:0, one launch (start us, length us, event | category | flops | bytes accessed | tf_op | source)
XLA Modules:
  0.0 91.4 jit_solution(11473663033753706618)
XLA Ops:
  1.3 0.7 copy-done.6
  2.0 0.1 shard_map.103
  2.1 0.5 collective-permute-start
  2.6 0.2 shard_map.104
  2.8 0.6 collective-permute-done.refs_1_
  3.4 2.9 %collective-permute-start.1 = (f32[8,128]{1,0:T(8,128)S(1)}, f32[8,128]{1,0:T(8,128)S(1)}, u32[]{:S(2)}, u32[]{:S(2)}) collective-permute-start(f32[8,128]{1,0:T(8,128)S(1)} %get-tuple-element.101.refs_0_), channel_id=1, source_target_pairs={{0,2},{1,3},{2,0},{3,1},{4,6},{5,7},{6,4},{7,5},{8,10},{9,11},{10,... | collective-permute-start | bytes 12296 | tf_op jit(solution)/shard_map/ppermute | solution.py:28
  6.3 1.3 %shard_map.106 = (f32[256,512]{1,0:T(8,128)S(1)}, f32[8,128]{1,0:T(8,128)S(1)}) custom-call(bf16[512,4096]{1,0:T(8,128)(2,1)S(1)} %bitcast.2, bf16[4096,256]{1,0:T(8,128)(2,1)S(1)} %copy-done.2, f32[8,128]{1,0:T(8,128)S(1)} %get-tuple-element.99.refs_2_), custom_call_target="tpu_custom_call" | custom-call | tf_op jit(solution)/shard_map/pallas_call | solution.py:66
  7.6 0.2 collective-permute-done.1.refs_1_
  7.9 2.1 %collective-permute-start.2 = (f32[8,128]{1,0:T(8,128)S(1)}, f32[8,128]{1,0:T(8,128)S(1)}, u32[]{:S(2)}, u32[]{:S(2)}) collective-permute-start(f32[8,128]{1,0:T(8,128)S(1)} %get-tuple-element.107.refs_4_), channel_id=1, source_target_pairs={{0,4},{1,5},{2,6},{3,7},{4,0},{5,1},{6,2},{7,3},{8,12},{9,13},{10,... | collective-permute-start | bytes 12296 | tf_op jit(solution)/shard_map/ppermute | solution.py:28
  10.0 1.3 %shard_map.108 = (f32[256,512]{1,0:T(8,128)S(1)}, f32[8,128]{1,0:T(8,128)S(1)}) custom-call(bf16[512,4096]{1,0:T(8,128)(2,1)S(1)} %bitcast.10, bf16[4096,256]{1,0:T(8,128)(2,1)S(1)} %copy-done.3, f32[8,128]{1,0:T(8,128)S(1)} %get-tuple-element.104.refs_2_), custom_call_target="tpu_custom_call" | custom-call | tf_op jit(solution)/shard_map/pallas_call | solution.py:66
  11.3 0.3 collective-permute-done.2.refs_5_
  11.6 0.2 shard_map.109
  11.8 0.5 shard_map.110
  12.3 0.1 collective-permute-start.3
  12.4 1.1 %shard_map.111 = (f32[8,152,128]{2,1,0:T(8,128)S(1)}, f32[8,136,128]{2,1,0:T(8,128)S(1)}, f32[8,128]{1,0:T(8,128)S(1)}) custom-call(bf16[512,4096]{1,0:T(8,128)(2,1)S(1)} %bitcast.4, bf16[512,4096]{1,0:T(8,128)(2,1)S(1)} %bitcast.12, bf16[256,512]{1,0:T(8,128)(2,1)S(1)} %get-tuple-element.111.refs_2_, bf16[256,512]{1,0:T(8,128)(2,1)S(1)} %get-tuple-element.112.refs_3_, ...), custom_call_target="tpu_custom_call" | custom-call | tf_op jit(solution)/shard_map/pallas_call | solution.py:66
  13.4 0.5 collective-permute-start.4
  13.9 0.5 collective-permute-done.3.refs_1_
  14.4 0.1 shard_map.112
  14.5 1.1 %shard_map.113 = (f32[8,136,128]{2,1,0:T(8,128)S(1)}, f32[8,128,128]{2,1,0:T(8,128)S(1)}, f32[8,128]{1,0:T(8,128)S(1)}) custom-call(bf16[512,4096]{1,0:T(8,128)(2,1)S(1)} %bitcast.5, bf16[512,4096]{1,0:T(8,128)(2,1)S(1)} %bitcast.13, bf16[256,512]{1,0:T(8,128)(2,1)S(1)} %get-tuple-element.111.refs_2_, bf16[256,512]{1,0:T(8,128)(2,1)S(1)} %get-tuple-element.112.refs_3_, ...), custom_call_target="tpu_custom_call" | custom-call | tf_op jit(solution)/shard_map/pallas_call | solution.py:66
  15.6 0.2 collective-permute-start.5
  15.8 0.1 shard_map.114
  15.9 2.1 %collective-permute-start.12 = (f32[8,136,128]{2,1,0:T(8,128)S(1)}, f32[8,136,128]{2,1,0:T(8,128)S(1)}, u32[]{:S(2)}, u32[]{:S(2)}) collective-permute-start(f32[8,136,128]{2,1,0:T(8,128)S(1)} %get-tuple-element.140), channel_id=1, source_target_pairs={{0,4},{1,5},{2,6},{3,7},{4,0},{5,1},{6,2},{7,3},{8,12},{9,13},{10,... | collective-permute-start | bytes 1671176 | tf_op jit(solution)/shard_map/ppermute | solution.py:28
  18.0 0.8 shard_map.115
  18.7 0.1 collective-permute-start.6
  18.9 0.1 shard_map.116
  18.9 0.5 shard_map.117
  19.4 1.1 %collective-permute-done.6.refs_1_ = f32[8,96,128]{2,1,0:T(8,128)S(1)} collective-permute-done((f32[8,96,128]{2,1,0:T(8,128)S(1)}, f32[8,96,128]{2,1,0:T(8,128)S(1)}, u32[]{:S(2)}, u32[]{:S(2)}) %collective-permute-start.6) | collective-permute-done | bytes 393248 | tf_op jit(solution)/shard_map/ppermute | solution.py:28
  20.5 0.1 shard_map.118
  20.6 1.7 %shard_map.119 = (f32[8,152,128]{2,1,0:T(8,128)S(1)}, f32[8,136,128]{2,1,0:T(8,128)S(1)}, f32[8,128,128]{2,1,0:T(8,128)S(1)}, f32[8,96,128]{2,1,0:T(8,128)S(1)}, f32[8,128]{1,0:T(8,128)S(1)}) custom-call(bf16[512,4096]{1,0:T(8,128)(2,1)S(1)} %bitcast.8, bf16[512,4096]{1,0:T(8,128)(2,1)S(1)} %bitcast.16, bf16[256,512]{1,0:T(8,128)(2,1)S(1)} %get-tuple-element.111.refs_2_, ...), custom_call_target="tpu_custom_call" | custom-call | tf_op jit(solution)/shard_map/pallas_call | solution.py:66
  22.3 0.2 collective-permute-start.11
  22.5 1.5 %collective-permute-start.10 = (f32[8,128,128]{2,1,0:T(8,128)S(1)}, f32[8,128,128]{2,1,0:T(8,128)S(1)}, u32[]{:S(2)}, u32[]{:S(2)}) collective-permute-start(f32[8,128,128]{2,1,0:T(8,128)S(1)} %get-tuple-element.137), channel_id=1, source_target_pairs={{0,2},{1,3},{2,0},{3,1},{4,6},{5,7},{6,4},{7,5},{8,10},{9,11},{10,... | collective-permute-start | bytes 1572872 | tf_op jit(solution)/shard_map/ppermute | solution.py:28
  24.0 1.6 %collective-permute-start.8 = (f32[8,152,128]{2,1,0:T(8,128)S(1)}, f32[8,152,128]{2,1,0:T(8,128)S(1)}, u32[]{:S(2)}, u32[]{:S(2)}) collective-permute-start(f32[8,152,128]{2,1,0:T(8,128)S(1)} %get-tuple-element.134), channel_id=1, source_target_pairs={{0,8},{1,9},{2,10},{3,11},{4,12},{5,13},{6,14},{7,15},{8,0},{9,1},... | collective-permute-start | bytes 1867784 | tf_op jit(solution)/shard_map/ppermute | solution.py:28
  25.5 5.6 %collective-permute-done.12.refs_2_ = f32[8,136,128]{2,1,0:T(8,128)S(1)} collective-permute-done((f32[8,136,128]{2,1,0:T(8,128)S(1)}, f32[8,136,128]{2,1,0:T(8,128)S(1)}, u32[]{:S(2)}, u32[]{:S(2)}) %collective-permute-start.12) | collective-permute-done | bytes 557088 | tf_op jit(solution)/shard_map/ppermute | solution.py:28
  31.1 5.6 %collective-permute-done.10.refs_2_ = f32[8,128,128]{2,1,0:T(8,128)S(1)} collective-permute-done((f32[8,128,128]{2,1,0:T(8,128)S(1)}, f32[8,128,128]{2,1,0:T(8,128)S(1)}, u32[]{:S(2)}, u32[]{:S(2)}) %collective-permute-start.10) | collective-permute-done | bytes 524320 | tf_op jit(solution)/shard_map/ppermute | solution.py:28
  36.7 2.6 %collective-permute-start.18 = (f32[8,96,128]{2,1,0:T(8,128)S(1)}, f32[8,96,128]{2,1,0:T(8,128)S(1)}, u32[]{:S(2)}, u32[]{:S(2)}) collective-permute-start(f32[8,96,128]{2,1,0:T(8,128)S(1)} %get-tuple-element.155), channel_id=1, source_target_pairs={{0,16},{1,17},{2,18},{3,19},{4,20},{5,21},{6,22},{7,23},{8,24},{9,... | collective-permute-start | bytes 1179656 | tf_op jit(solution)/shard_map/ppermute | solution.py:28
  39.3 1.7 %shard_map.120 = (f32[8,152,128]{2,1,0:T(8,128)S(1)}, f32[8,136,128]{2,1,0:T(8,128)S(1)}, f32[8,128,128]{2,1,0:T(8,128)S(1)}, f32[8,96,128]{2,1,0:T(8,128)S(1)}, f32[8,128]{1,0:T(8,128)S(1)}) custom-call(bf16[512,4096]{1,0:T(8,128)(2,1)S(1)} %bitcast.9, bf16[512,4096]{1,0:T(8,128)(2,1)S(1)} %bitcast.17, bf16[256,512]{1,0:T(8,128)(2,1)S(1)} %get-tuple-element.111.refs_2_, ...), custom_call_target="tpu_custom_call" | custom-call | tf_op jit(solution)/shard_map/pallas_call | solution.py:66
  41.0 0.1 shard_map.121
  41.1 0.1 shard_map.122
  41.2 0.6 collective-permute-start.14
  41.8 0.1 shard_map.123
  41.9 1.6 %collective-permute-start.13 = (f32[4,152,128]{2,1,0:T(8,128)S(1)}, f32[4,152,128]{2,1,0:T(8,128)S(1)}, u32[]{:S(2)}, u32[]{:S(2)}) collective-permute-start(f32[4,152,128]{2,1,0:T(8,128)S(1)} %get-tuple-element.145), channel_id=1, source_target_pairs={{0,2},{1,3},{2,0},{3,1},{4,6},{5,7},{6,4},{7,5},{8,10},{9,11},{10,... | collective-permute-start | bytes 933896 | tf_op jit(solution)/shard_map/ppermute | solution.py:28
  43.4 0.5 collective-permute-start.16
  44.0 6.0 %collective-permute-done.14.refs_1_ = f32[4,128,128]{2,1,0:T(8,128)S(1)} collective-permute-done((f32[4,128,128]{2,1,0:T(8,128)S(1)}, f32[4,128,128]{2,1,0:T(8,128)S(1)}, u32[]{:S(2)}, u32[]{:S(2)}) %collective-permute-start.14) | collective-permute-done | bytes 262176 | tf_op jit(solution)/shard_map/ppermute | solution.py:28
  50.0 1.6 %collective-permute-start.15 = (f32[2,128,128]{2,1,0:T(8,128)S(1)}, f32[2,128,128]{2,1,0:T(8,128)S(1)}, u32[]{:S(2)}, u32[]{:S(2)}) collective-permute-start(f32[2,128,128]{2,1,0:T(8,128)S(1)} %get-tuple-element.150), channel_id=1, source_target_pairs={{0,8},{1,9},{2,10},{3,11},{4,12},{5,13},{6,14},{7,15},{8,0},{9,1},... | collective-permute-start | bytes 393224 | tf_op jit(solution)/shard_map/ppermute | solution.py:28
  51.7 5.0 %collective-permute-done.18.refs_2_ = f32[8,96,128]{2,1,0:T(8,128)S(1)} collective-permute-done((f32[8,96,128]{2,1,0:T(8,128)S(1)}, f32[8,96,128]{2,1,0:T(8,128)S(1)}, u32[]{:S(2)}, u32[]{:S(2)}) %collective-permute-start.18) | collective-permute-done | bytes 393248 | tf_op jit(solution)/shard_map/ppermute | solution.py:28
  56.7 0.1 shard_map.125
  56.8 0.5 collective-permute-start.21
  57.3 0.1 collective-permute-done.16.refs_1_
  57.5 2.0 %collective-permute-done.15.refs_1_ = f32[2,128,128]{2,1,0:T(8,128)S(1)} collective-permute-done((f32[2,128,128]{2,1,0:T(8,128)S(1)}, f32[2,128,128]{2,1,0:T(8,128)S(1)}, u32[]{:S(2)}, u32[]{:S(2)}) %collective-permute-start.15) | collective-permute-done | bytes 131104 | tf_op jit(solution)/shard_map/ppermute | solution.py:28
  59.5 0.5 collective-permute-start.19
  60.0 0.7 collective-permute-start.20
  60.7 2.2 %collective-permute-done.21.refs_1_ = f32[4,96,128]{2,1,0:T(8,128)S(1)} collective-permute-done((f32[4,96,128]{2,1,0:T(8,128)S(1)}, f32[4,96,128]{2,1,0:T(8,128)S(1)}, u32[]{:S(2)}, u32[]{:S(2)}) %collective-permute-start.21) | collective-permute-done | bytes 196640 | tf_op jit(solution)/shard_map/ppermute | solution.py:28
  62.9 2.4 %collective-permute-start.22 = (f32[2,96,128]{2,1,0:T(8,128)S(1)}, f32[2,96,128]{2,1,0:T(8,128)S(1)}, u32[]{:S(2)}, u32[]{:S(2)}) collective-permute-start(f32[2,96,128]{2,1,0:T(8,128)S(1)} %get-tuple-element.173), channel_id=1, source_target_pairs={{0,8},{1,9},{2,10},{3,11},{4,12},{5,13},{6,14},{7,15},{8,0},{9,1},... | collective-permute-start | bytes 294920 | tf_op jit(solution)/shard_map/ppermute | solution.py:28
  65.3 1.0 %collective-permute-done.20.refs_1_ = f32[2,136,128]{2,1,0:T(8,128)S(1)} collective-permute-done((f32[2,136,128]{2,1,0:T(8,128)S(1)}, f32[2,136,128]{2,1,0:T(8,128)S(1)}, u32[]{:S(2)}, u32[]{:S(2)}) %collective-permute-start.20) | collective-permute-done | bytes 139296 | tf_op jit(solution)/shard_map/ppermute | solution.py:28
  66.5 2.5 %collective-permute-start.23 = (f32[1,152,128]{2,1,0:T(8,128)S(1)}, f32[1,152,128]{2,1,0:T(8,128)S(1)}, u32[]{:S(2)}, u32[]{:S(2)}) collective-permute-start(f32[1,152,128]{2,1,0:T(8,128)S(1)} %get-tuple-element.176), channel_id=1, source_target_pairs={{0,16},{1,17},{2,18},{3,19},{4,20},{5,21},{6,22},{7,23},{8,24},{9,... | collective-permute-start | bytes 233480 | tf_op jit(solution)/shard_map/ppermute | solution.py:28
  68.9 0.5 collective-permute-start.24
  69.4 2.4 %collective-permute-start.25 = (f32[1,128,128]{2,1,0:T(8,128)S(1)}, f32[1,128,128]{2,1,0:T(8,128)S(1)}, u32[]{:S(2)}, u32[]{:S(2)}) collective-permute-start(f32[1,128,128]{2,1,0:T(8,128)S(1)} %get-tuple-element.178), channel_id=1, source_target_pairs={{0,16},{1,17},{2,18},{3,19},{4,20},{5,21},{6,22},{7,23},{8,24},{9,... | collective-permute-start | bytes 196616 | tf_op jit(solution)/shard_map/ppermute | solution.py:28
  71.8 1.5 %collective-permute-start.26 = (f32[1,96,128]{2,1,0:T(8,128)S(1)}, f32[1,96,128]{2,1,0:T(8,128)S(1)}, u32[]{:S(2)}, u32[]{:S(2)}) collective-permute-start(f32[1,96,128]{2,1,0:T(8,128)S(1)} %get-tuple-element.179), channel_id=1, source_target_pairs={{0,2},{1,3},{2,0},{3,1},{4,6},{5,7},{6,4},{7,5},{8,10},{9,11},{10,... | collective-permute-start | bytes 147464 | tf_op jit(solution)/shard_map/ppermute | solution.py:28
  73.4 5.2 %collective-permute-done.25.refs_6_ = f32[1,128,128]{2,1,0:T(8,128)S(1)} collective-permute-done((f32[1,128,128]{2,1,0:T(8,128)S(1)}, f32[1,128,128]{2,1,0:T(8,128)S(1)}, u32[]{:S(2)}, u32[]{:S(2)}) %collective-permute-start.25) | collective-permute-done | bytes 65568 | tf_op jit(solution)/shard_map/ppermute | solution.py:28
  78.5 0.7 shard_map.133
  79.2 4.2 %all-to-all-start = ((f32[32,1,128]{2,1,0:T(1,128)}), f32[32,1,128]{2,1,0:T(1,128)S(1)}, u32[]{:S(2)}, u32[]{:S(2)}) async-start(f32[32,1,128]{2,1,0:T(1,128)} %get-tuple-element.183), calls=%async_computation | async-start | bytes 32768 | tf_op jit(solution)/shard_map/all_to_all | solution.py:326
  83.4 0.6 copy.11
  84.0 6.5 %all-to-all-done.refs_2_ = f32[32,1,128]{2,1,0:T(1,128)S(1)} async-done(((f32[32,1,128]{2,1,0:T(1,128)}), f32[32,1,128]{2,1,0:T(1,128)S(1)}, u32[]{:S(2)}, u32[]{:S(2)}) %all-to-all-start) | async-done | bytes 16416 | tf_op jit(solution)/shard_map/all_to_all | solution.py:326
  90.5 0.9 %shard_map.134 = (f32[128,256]{1,0:T(8,128)}, f32[128,256]{1,0:T(8,128)}, f32[8,128]{1,0:T(8,128)}) custom-call(f32[256,128]{1,0:T(8,128)S(1)} %get-tuple-element.181.refs_0_, f32[256,128]{1,0:T(8,128)S(1)} %get-tuple-element.182.refs_1_, f32[32,1,128]{2,1,0:T(1,128)S(1)} %all-to-all-done.refs_2_, f32[8,128]{1,0:T(8,128)S(1)} %get-tuple-element.184.refs_3_), custom_call_target="tpu_custom_call" | custom-call | tf_op jit(solution)/shard_map/pallas_call | solution.py:66
  (40 shorter events, 0.3 us)
Async XLA Ops:
  1.3 0.7 copy-start.6
  2.1 1.3 %collective-permute-start = (f32[8,128]{1,0:T(8,128)S(1)}, f32[8,128]{1,0:T(8,128)S(1)}, u32[]{:S(2)}, u32[]{:S(2)}) collective-permute-start(f32[8,128]{1,0:T(8,128)S(1)} %get-tuple-element.95.refs_0_), channel_id=1, source_target_pairs={{0,1},{1,0},{2,3},{3,2},{4,5},{5,4},{6,7},{7,6},{8,9},{9,8},{10,11... | collective-permute-start | bytes 12296 | tf_op jit(solution)/shard_map/ppermute | solution.py:28
  2.6 3.7 %copy-start = (bf16[1,512,4096]{2,1,0:T(8,128)(2,1)S(1)}, bf16[1,512,4096]{2,1,0:T(8,128)(2,1)}, u32[]{:S(2)}) copy-start(bf16[1,512,4096]{2,1,0:T(8,128)(2,1)} %param.8) | copy-start | bytes 12582916
  2.6 3.7 %copy-start.2 = (bf16[4096,256]{1,0:T(8,128)(2,1)S(1)}, bf16[4096,256]{1,0:T(8,128)(2,1)}, u32[]{:S(2)}) copy-start(bf16[4096,256]{1,0:T(8,128)(2,1)} %refs_1_.4) | copy-start | bytes 6291460
  2.8 7.2 %copy-start.1 = (bf16[1,512,4096]{2,1,0:T(8,128)(2,1)S(1)}, bf16[1,512,4096]{2,1,0:T(8,128)(2,1)}, u32[]{:S(2)}) copy-start(bf16[1,512,4096]{2,1,0:T(8,128)(2,1)} %param.9) | copy-start | bytes 12582916
  2.8 7.2 %copy-start.3 = (bf16[4096,256]{1,0:T(8,128)(2,1)S(1)}, bf16[4096,256]{1,0:T(8,128)(2,1)}, u32[]{:S(2)}) copy-start(bf16[4096,256]{1,0:T(8,128)(2,1)} %refs_1_.5) | copy-start | bytes 6291460
  3.4 4.5 %collective-permute-start.1 = (f32[8,128]{1,0:T(8,128)S(1)}, f32[8,128]{1,0:T(8,128)S(1)}, u32[]{:S(2)}, u32[]{:S(2)}) collective-permute-start(f32[8,128]{1,0:T(8,128)S(1)} %get-tuple-element.101.refs_0_), channel_id=1, source_target_pairs={{0,2},{1,3},{2,0},{3,1},{4,6},{5,7},{6,4},{7,5},{8,10},{9,11},{10,... | collective-permute-start | bytes 12296 | tf_op jit(solution)/shard_map/ppermute | solution.py:28
  7.6 4.0 %copy-start.4 = (f32[1,512]{1,0:T(1,128)S(1)}, f32[1,512]{1,0:T(1,128)}, u32[]{:S(2)}) copy-start(f32[1,512]{1,0:T(1,128)} %refs_7_.1) | copy-start | bytes 6148
  7.6 4.0 %copy-start.5 = (f32[1,512]{1,0:T(1,128)S(1)}, f32[1,512]{1,0:T(1,128)}, u32[]{:S(2)}) copy-start(f32[1,512]{1,0:T(1,128)} %refs_8_.1) | copy-start | bytes 6148
  7.9 3.7 %collective-permute-start.2 = (f32[8,128]{1,0:T(8,128)S(1)}, f32[8,128]{1,0:T(8,128)S(1)}, u32[]{:S(2)}, u32[]{:S(2)}) collective-permute-start(f32[8,128]{1,0:T(8,128)S(1)} %get-tuple-element.107.refs_4_), channel_id=1, source_target_pairs={{0,4},{1,5},{2,6},{3,7},{4,0},{5,1},{6,2},{7,3},{8,12},{9,13},{10,... | collective-permute-start | bytes 12296 | tf_op jit(solution)/shard_map/ppermute | solution.py:28
  12.3 2.1 %collective-permute-start.3 = (f32[8,152,128]{2,1,0:T(8,128)S(1)}, f32[8,152,128]{2,1,0:T(8,128)S(1)}, u32[]{:S(2)}, u32[]{:S(2)}) collective-permute-start(f32[8,152,128]{2,1,0:T(8,128)S(1)} %get-tuple-element.116), channel_id=1, source_target_pairs={{0,1},{1,0},{2,3},{3,2},{4,5},{5,4},{6,7},{7,6},{8,9},{9,8},{10,11... | collective-permute-start | bytes 1867784 | tf_op jit(solution)/shard_map/ppermute | solution.py:28
  13.4 2.4 %collective-permute-start.4 = (f32[8,136,128]{2,1,0:T(8,128)S(1)}, f32[8,136,128]{2,1,0:T(8,128)S(1)}, u32[]{:S(2)}, u32[]{:S(2)}) collective-permute-start(f32[8,136,128]{2,1,0:T(8,128)S(1)} %get-tuple-element.120), channel_id=1, source_target_pairs={{0,1},{1,0},{2,3},{3,2},{4,5},{5,4},{6,7},{7,6},{8,9},{9,8},{10,11... | collective-permute-start | bytes 1671176 | tf_op jit(solution)/shard_map/ppermute | solution.py:28
  15.6 3.3 %collective-permute-start.5 = (f32[8,128,128]{2,1,0:T(8,128)S(1)}, f32[8,128,128]{2,1,0:T(8,128)S(1)}, u32[]{:S(2)}, u32[]{:S(2)}) collective-permute-start(f32[8,128,128]{2,1,0:T(8,128)S(1)} %get-tuple-element.124), channel_id=1, source_target_pairs={{0,1},{1,0},{2,3},{3,2},{4,5},{5,4},{6,7},{7,6},{8,9},{9,8},{10,11... | collective-permute-start | bytes 1572872 | tf_op jit(solution)/shard_map/ppermute | solution.py:28
  15.9 15.2 %collective-permute-start.12 = (f32[8,136,128]{2,1,0:T(8,128)S(1)}, f32[8,136,128]{2,1,0:T(8,128)S(1)}, u32[]{:S(2)}, u32[]{:S(2)}) collective-permute-start(f32[8,136,128]{2,1,0:T(8,128)S(1)} %get-tuple-element.140), channel_id=1, source_target_pairs={{0,4},{1,5},{2,6},{3,7},{4,0},{5,1},{6,2},{7,3},{8,12},{9,13},{10,... | collective-permute-start | bytes 1671176 | tf_op jit(solution)/shard_map/ppermute | solution.py:28
  18.7 1.8 %collective-permute-start.6 = (f32[8,96,128]{2,1,0:T(8,128)S(1)}, f32[8,96,128]{2,1,0:T(8,128)S(1)}, u32[]{:S(2)}, u32[]{:S(2)}) collective-permute-start(f32[8,96,128]{2,1,0:T(8,128)S(1)} %get-tuple-element.128), channel_id=1, source_target_pairs={{0,1},{1,0},{2,3},{3,2},{4,5},{5,4},{6,7},{7,6},{8,9},{9,8},{10,11... | collective-permute-start | bytes 1179656 | tf_op jit(solution)/shard_map/ppermute | solution.py:28
  22.3 17.0 %collective-permute-start.11 = (f32[8,136,128]{2,1,0:T(8,128)S(1)}, f32[8,136,128]{2,1,0:T(8,128)S(1)}, u32[]{:S(2)}, u32[]{:S(2)}) collective-permute-start(f32[8,136,128]{2,1,0:T(8,128)S(1)} %get-tuple-element.139), channel_id=1, source_target_pairs={{0,1},{1,0},{2,3},{3,2},{4,5},{5,4},{6,7},{7,6},{8,9},{9,8},{10,11... | collective-permute-start | bytes 1671176 | tf_op jit(solution)/shard_map/ppermute | solution.py:28
  22.5 14.2 %collective-permute-start.10 = (f32[8,128,128]{2,1,0:T(8,128)S(1)}, f32[8,128,128]{2,1,0:T(8,128)S(1)}, u32[]{:S(2)}, u32[]{:S(2)}) collective-permute-start(f32[8,128,128]{2,1,0:T(8,128)S(1)} %get-tuple-element.137), channel_id=1, source_target_pairs={{0,2},{1,3},{2,0},{3,1},{4,6},{5,7},{6,4},{7,5},{8,10},{9,11},{10,... | collective-permute-start | bytes 1572872 | tf_op jit(solution)/shard_map/ppermute | solution.py:28
  24.0 17.8 %collective-permute-start.8 = (f32[8,152,128]{2,1,0:T(8,128)S(1)}, f32[8,152,128]{2,1,0:T(8,128)S(1)}, u32[]{:S(2)}, u32[]{:S(2)}) collective-permute-start(f32[8,152,128]{2,1,0:T(8,128)S(1)} %get-tuple-element.134), channel_id=1, source_target_pairs={{0,8},{1,9},{2,10},{3,11},{4,12},{5,13},{6,14},{7,15},{8,0},{9,1},... | collective-permute-start | bytes 1867784 | tf_op jit(solution)/shard_map/ppermute | solution.py:28
  25.5 16.2 %collective-permute-start.7 = (f32[8,152,128]{2,1,0:T(8,128)S(1)}, f32[8,152,128]{2,1,0:T(8,128)S(1)}, u32[]{:S(2)}, u32[]{:S(2)}) collective-permute-start(f32[8,152,128]{2,1,0:T(8,128)S(1)} %get-tuple-element.133), channel_id=1, source_target_pairs={{0,1},{1,0},{2,3},{3,2},{4,5},{5,4},{6,7},{7,6},{8,9},{9,8},{10,11... | collective-permute-start | bytes 1867784 | tf_op jit(solution)/shard_map/ppermute | solution.py:28
  31.1 10.0 %collective-permute-start.9 = (f32[8,128,128]{2,1,0:T(8,128)S(1)}, f32[8,128,128]{2,1,0:T(8,128)S(1)}, u32[]{:S(2)}, u32[]{:S(2)}) collective-permute-start(f32[8,128,128]{2,1,0:T(8,128)S(1)} %get-tuple-element.136), channel_id=1, source_target_pairs={{0,1},{1,0},{2,3},{3,2},{4,5},{5,4},{6,7},{7,6},{8,9},{9,8},{10,11... | collective-permute-start | bytes 1572872 | tf_op jit(solution)/shard_map/ppermute | solution.py:28
  36.7 20.0 %collective-permute-start.18 = (f32[8,96,128]{2,1,0:T(8,128)S(1)}, f32[8,96,128]{2,1,0:T(8,128)S(1)}, u32[]{:S(2)}, u32[]{:S(2)}) collective-permute-start(f32[8,96,128]{2,1,0:T(8,128)S(1)} %get-tuple-element.155), channel_id=1, source_target_pairs={{0,16},{1,17},{2,18},{3,19},{4,20},{5,21},{6,22},{7,23},{8,24},{9,... | collective-permute-start | bytes 1179656 | tf_op jit(solution)/shard_map/ppermute | solution.py:28
  39.3 17.4 %collective-permute-start.17 = (f32[8,96,128]{2,1,0:T(8,128)S(1)}, f32[8,96,128]{2,1,0:T(8,128)S(1)}, u32[]{:S(2)}, u32[]{:S(2)}) collective-permute-start(f32[8,96,128]{2,1,0:T(8,128)S(1)} %get-tuple-element.154), channel_id=1, source_target_pairs={{0,1},{1,0},{2,3},{3,2},{4,5},{5,4},{6,7},{7,6},{8,9},{9,8},{10,11... | collective-permute-start | bytes 1179656 | tf_op jit(solution)/shard_map/ppermute | solution.py:28
  41.2 8.8 %collective-permute-start.14 = (f32[4,128,128]{2,1,0:T(8,128)S(1)}, f32[4,128,128]{2,1,0:T(8,128)S(1)}, u32[]{:S(2)}, u32[]{:S(2)}) collective-permute-start(f32[4,128,128]{2,1,0:T(8,128)S(1)} %get-tuple-element.147), channel_id=1, source_target_pairs={{0,4},{1,5},{2,6},{3,7},{4,0},{5,1},{6,2},{7,3},{8,12},{9,13},{10,... | collective-permute-start | bytes 786440 | tf_op jit(solution)/shard_map/ppermute | solution.py:28
  41.9 17.6 %collective-permute-start.13 = (f32[4,152,128]{2,1,0:T(8,128)S(1)}, f32[4,152,128]{2,1,0:T(8,128)S(1)}, u32[]{:S(2)}, u32[]{:S(2)}) collective-permute-start(f32[4,152,128]{2,1,0:T(8,128)S(1)} %get-tuple-element.145), channel_id=1, source_target_pairs={{0,2},{1,3},{2,0},{3,1},{4,6},{5,7},{6,4},{7,5},{8,10},{9,11},{10,... | collective-permute-start | bytes 933896 | tf_op jit(solution)/shard_map/ppermute | solution.py:28
  43.4 14.0 %collective-permute-start.16 = (f32[4,136,128]{2,1,0:T(8,128)S(1)}, f32[4,136,128]{2,1,0:T(8,128)S(1)}, u32[]{:S(2)}, u32[]{:S(2)}) collective-permute-start(f32[4,136,128]{2,1,0:T(8,128)S(1)} %get-tuple-element.152), channel_id=1, source_target_pairs={{0,2},{1,3},{2,0},{3,1},{4,6},{5,7},{6,4},{7,5},{8,10},{9,11},{10,... | collective-permute-start | bytes 835592 | tf_op jit(solution)/shard_map/ppermute | solution.py:28
  50.0 9.4 %collective-permute-start.15 = (f32[2,128,128]{2,1,0:T(8,128)S(1)}, f32[2,128,128]{2,1,0:T(8,128)S(1)}, u32[]{:S(2)}, u32[]{:S(2)}) collective-permute-start(f32[2,128,128]{2,1,0:T(8,128)S(1)} %get-tuple-element.150), channel_id=1, source_target_pairs={{0,8},{1,9},{2,10},{3,11},{4,12},{5,13},{6,14},{7,15},{8,0},{9,1},... | collective-permute-start | bytes 393224 | tf_op jit(solution)/shard_map/ppermute | solution.py:28
  56.8 6.1 %collective-permute-start.21 = (f32[4,96,128]{2,1,0:T(8,128)S(1)}, f32[4,96,128]{2,1,0:T(8,128)S(1)}, u32[]{:S(2)}, u32[]{:S(2)}) collective-permute-start(f32[4,96,128]{2,1,0:T(8,128)S(1)} %get-tuple-element.165), channel_id=1, source_target_pairs={{0,4},{1,5},{2,6},{3,7},{4,0},{5,1},{6,2},{7,3},{8,12},{9,13},{10,... | collective-permute-start | bytes 589832 | tf_op jit(solution)/shard_map/ppermute | solution.py:28
  59.5 6.9 %collective-permute-start.19 = (f32[2,152,128]{2,1,0:T(8,128)S(1)}, f32[2,152,128]{2,1,0:T(8,128)S(1)}, u32[]{:S(2)}, u32[]{:S(2)}) collective-permute-start(f32[2,152,128]{2,1,0:T(8,128)S(1)} %get-tuple-element.161), channel_id=1, source_target_pairs={{0,4},{1,5},{2,6},{3,7},{4,0},{5,1},{6,2},{7,3},{8,12},{9,13},{10,... | collective-permute-start | bytes 466952 | tf_op jit(solution)/shard_map/ppermute | solution.py:28
  60.0 6.4 %collective-permute-start.20 = (f32[2,136,128]{2,1,0:T(8,128)S(1)}, f32[2,136,128]{2,1,0:T(8,128)S(1)}, u32[]{:S(2)}, u32[]{:S(2)}) collective-permute-start(f32[2,136,128]{2,1,0:T(8,128)S(1)} %get-tuple-element.163), channel_id=1, source_target_pairs={{0,8},{1,9},{2,10},{3,11},{4,12},{5,13},{6,14},{7,15},{8,0},{9,1},... | collective-permute-start | bytes 417800 | tf_op jit(solution)/shard_map/ppermute | solution.py:28
  62.9 8.9 %collective-permute-start.22 = (f32[2,96,128]{2,1,0:T(8,128)S(1)}, f32[2,96,128]{2,1,0:T(8,128)S(1)}, u32[]{:S(2)}, u32[]{:S(2)}) collective-permute-start(f32[2,96,128]{2,1,0:T(8,128)S(1)} %get-tuple-element.173), channel_id=1, source_target_pairs={{0,8},{1,9},{2,10},{3,11},{4,12},{5,13},{6,14},{7,15},{8,0},{9,1},... | collective-permute-start | bytes 294920 | tf_op jit(solution)/shard_map/ppermute | solution.py:28
  66.5 12.1 %collective-permute-start.23 = (f32[1,152,128]{2,1,0:T(8,128)S(1)}, f32[1,152,128]{2,1,0:T(8,128)S(1)}, u32[]{:S(2)}, u32[]{:S(2)}) collective-permute-start(f32[1,152,128]{2,1,0:T(8,128)S(1)} %get-tuple-element.176), channel_id=1, source_target_pairs={{0,16},{1,17},{2,18},{3,19},{4,20},{5,21},{6,22},{7,23},{8,24},{9,... | collective-permute-start | bytes 233480 | tf_op jit(solution)/shard_map/ppermute | solution.py:28
  68.9 9.6 %collective-permute-start.24 = (f32[1,136,128]{2,1,0:T(8,128)S(1)}, f32[1,136,128]{2,1,0:T(8,128)S(1)}, u32[]{:S(2)}, u32[]{:S(2)}) collective-permute-start(f32[1,136,128]{2,1,0:T(8,128)S(1)} %get-tuple-element.177), channel_id=1, source_target_pairs={{0,16},{1,17},{2,18},{3,19},{4,20},{5,21},{6,22},{7,23},{8,24},{9,... | collective-permute-start | bytes 208904 | tf_op jit(solution)/shard_map/ppermute | solution.py:28
  69.4 9.1 %collective-permute-start.25 = (f32[1,128,128]{2,1,0:T(8,128)S(1)}, f32[1,128,128]{2,1,0:T(8,128)S(1)}, u32[]{:S(2)}, u32[]{:S(2)}) collective-permute-start(f32[1,128,128]{2,1,0:T(8,128)S(1)} %get-tuple-element.178), channel_id=1, source_target_pairs={{0,16},{1,17},{2,18},{3,19},{4,20},{5,21},{6,22},{7,23},{8,24},{9,... | collective-permute-start | bytes 196616 | tf_op jit(solution)/shard_map/ppermute | solution.py:28
  71.8 6.7 %collective-permute-start.26 = (f32[1,96,128]{2,1,0:T(8,128)S(1)}, f32[1,96,128]{2,1,0:T(8,128)S(1)}, u32[]{:S(2)}, u32[]{:S(2)}) collective-permute-start(f32[1,96,128]{2,1,0:T(8,128)S(1)} %get-tuple-element.179), channel_id=1, source_target_pairs={{0,2},{1,3},{2,0},{3,1},{4,6},{5,7},{6,4},{7,5},{8,10},{9,11},{10,... | collective-permute-start | bytes 147464 | tf_op jit(solution)/shard_map/ppermute | solution.py:28
  79.2 11.3 %all-to-all-start = ((f32[32,1,128]{2,1,0:T(1,128)}), f32[32,1,128]{2,1,0:T(1,128)S(1)}, u32[]{:S(2)}, u32[]{:S(2)}) async-start(f32[32,1,128]{2,1,0:T(1,128)} %get-tuple-element.183), calls=%async_computation | async-start | bytes 32768 | tf_op jit(solution)/shard_map/all_to_all | solution.py:326

commit v2 on v1

--- a/solution.py
+++ b/solution.py
@@ -16,8 +16,8 @@
 KERNEL_VMEM = 8 * 1024 * 1024
 F32 = jnp.float32
 
-PARTS = (("zxyw", 19), ("yxzw", 17), ("xyzw", 16), ("wyzx", 12))
-TURNS = (1, 2, 0, 2, 3, 1, 2, 0, 3, 1, 0, 3)
+PARTS = (("yxzw", "xyzw", 16), ("xzwy", "yzwx", 14), ("zyxw", "zxyw", 19), ("xyzw", "yxzw", 15))
+TURNS = (0, 1, 3, 2, 0, 1, 3, 2, 0, 2, 3, 1)
 
 SMEM = pl.BlockSpec(memory_space=pltpu.SMEM)
 VMEM = pl.BlockSpec(memory_space=pltpu.VMEM)
@@ -25,7 +25,8 @@
 
 
 def swap(x, mask, count):
-    return lax.ppermute(x, AXES, [(i, i ^ mask) for i in range(count)])
+    even, odd = mask if isinstance(mask, tuple) else (mask, mask)
+    return lax.ppermute(x, AXES, [(i, i ^ (odd if i & 1 else even)) for i in range(count)])
 
 
 class Line:
@@ -148,12 +149,14 @@
 def blocks_body(*refs, jobs, seq_size):
     hid, direction, scaled_up, scaled_down, *outs = refs
     me = lax.axis_index("batch") * seq_size + lax.axis_index("seq")
+    odd = me & 1
     for out_at, tiles, row_at, rows, side, from_row in jobs:
         src, weight = ((hid, scaled_up), (direction, scaled_down))[side]
         out = outs[out_at]
         for i in range(0, len(tiles), 2):
             pair = tiles[i : i + 2]
-            cols = [src[:, pl.ds(pl.multiple_of((t ^ me) * LANES, LANES), LANES)] for t in pair]
+            names = [even + odd * (other - even) for even, other in pair]
+            cols = [src[:, pl.ds(pl.multiple_of((t ^ me) * LANES, LANES), LANES)] for t in names]
             block = jnp.concatenate(cols, axis=1) if len(cols) > 1 else cols[0]
             grad = jnp.dot(weight[from_row : from_row + rows, :], block, preferred_element_type=F32)
             for j in range(len(pair)):
@@ -283,8 +286,8 @@
     zs = [ns << j for j in range(log2(nb))]
     masks = {"x": plane[: len(plane) // 2], "y": plane[len(plane) // 2 :], "z": zs[:-1], "w": zs[-1:]}
     orders, pieces, at = [], [], 0
-    for axes, share in PARTS:
-        orders.append([m for axis in axes for m in masks[axis]])
+    for even, odd, share in PARTS:
+        orders.append([[m for axis in axes for m in masks[axis]] for axes in (even, odd)])
         end = at + 2 * rank * share // 64
         pieces.append([
             (side, max(at - side * rank, 0), min(end, rank * (side + 1)) - max(at, rank * side))
@@ -293,11 +296,11 @@
         ])
         at = end
     n = len(PARTS)
-    sends = [(tiles_of(orders[i][1:], orders[i][0]), pieces[i]) for i in range(n)]
-    stays = [(tiles_of(orders[i][1:], 0), pieces[i]) for i in range(n)]
-    far = lambda w: ([t | core for t in w[0]], w[1])
+    sends = [(list(zip(*[tiles_of(o[1:], o[0]) for o in orders[i]])), pieces[i]) for i in range(n)]
+    stays = [(list(zip(*[tiles_of(o[1:], 0) for o in orders[i]])), pieces[i]) for i in range(n)]
+    far = lambda w: ([(odd | core, even | core) for even, odd in w[0]], w[1])
     got, near, sent, kept = [None] * n, [None] * n, [None] * n, [None] * n
-    for name, i, k in script(len(orders[0])):
+    for name, i, k in script(len(orders[0][0])):
         if name == "blocks":
             want = ([sends[i - 1]] if i else []) + ([far(sends[i])] if i < n else [])
             made = list(blocks(line, ops, want, ns))
@@ -317,7 +320,7 @@
                 blocks_now, rows, _ = terms[0].shape
                 send, left = line.call(fold_body, [((blocks_now // 2, rows, LANES), F32)] * 2, terms)
                 kept[i] = (left,)
-            sent[i] = swap(send, orders[i][k], count)
+            sent[i] = swap(send, tuple(o[k] for o in orders[i]), count)
 
     down, up, squares = line.call(
         functools.partial(total_body, n=n, rank=rank),

time: 91.6 us -> 86.9 us (0.949)
  waiting for transfers between devices: 41.9 us -> 33.8 us
  starting transfers between devices: 33.9 us -> 37.3 us
    ppermute x27, waiting for transfers between devices: 35.3 us -> 27.3 us  [swap(): lax.ppermute(x, AXES, [(i, i ^ (odd if i & 1 else even)) for i in range(c...]
    ppermute x27, starting transfers between devices: 29.7 us -> 32.1 us  [swap(): lax.ppermute(x, AXES, [(i, i ^ (odd if i & 1 else even)) for i in range(c...]
    all_to_all x1, starting transfers between devices: 4.19 us -> 5.19 us  [in_blocks(): squares = lax.all_to_all(squares, AXES, 0, 0, tiled=True)]
  transfers between devices with their start and end apart: 28 -> 28, of which waited for: 15 -> 13; matrix products, arithmetic and copies ran while one was open for 1% -> 1% of each run, Pallas kernels for 12% -> 12%
where the time goes in v2:
time: 86.9 us; the launch traced here: 86.7 us
  starting transfers between devices  37.3 us (43%)
  waiting for transfers between devices  33.8 us (39%)
  Pallas kernels  12.8 us (15%)
  between operations  1.51 us (2%)
  local copies, waits for them, and re-layouts  1.29 us (1%)
    ppermute x27, starting transfers between devices, swap(): lax.ppermute(x, AXES, [(i, i ^ (odd if i & 1 else even)) for i in range(c...  32.1 us
    ppermute x27, waiting for transfers between devices, swap(): lax.ppermute(x, AXES, [(i, i ^ (odd if i & 1 else even)) for i in range(c...  27.3 us
    pallas_call x32, Pallas kernels, call(): *got, self.token = kernel(*scalars, *from_hbm, *ins)  12.8 us
    all_to_all x1, waiting for transfers between devices, in_blocks(): squares = lax.all_to_all(squares, AXES, 0, 0, tiled=True)  6.52 us
    all_to_all x1, starting transfers between devices, in_blocks(): squares = lax.all_to_all(squares, AXES, 0, 0, tiled=True)  5.19 us
  transfers between devices with their start and end apart: 28, of which 13 were waited for; matrix products, arithmetic and copies ran while one was open for 1% of the time, Pallas kernels for 12%

profile of v2, /device:TPU:0, one launch (start us, length us, event | category | flops | bytes accessed | tf_op | source)
XLA Modules:
  0.0 86.7 jit_solution(3701007406939071986)
XLA Ops:
  1.3 0.7 copy-done.6
  2.0 0.1 shard_map.103
  2.1 0.5 collective-permute-start
  2.6 0.2 shard_map.104
  2.8 0.6 collective-permute-done.refs_1_
  3.4 2.9 %collective-permute-start.1 = (f32[8,128]{1,0:T(8,128)S(1)}, f32[8,128]{1,0:T(8,128)S(1)}, u32[]{:S(2)}, u32[]{:S(2)}) collective-permute-start(f32[8,128]{1,0:T(8,128)S(1)} %get-tuple-element.101.refs_0_), channel_id=1, source_target_pairs={{0,2},{1,3},{2,0},{3,1},{4,6},{5,7},{6,4},{7,5},{8,10},{9,11},{10,... | collective-permute-start | bytes 12296 | tf_op jit(solution)/shard_map/ppermute | solution.py:29
  6.3 1.3 %shard_map.106 = (f32[256,512]{1,0:T(8,128)S(1)}, f32[8,128]{1,0:T(8,128)S(1)}) custom-call(bf16[512,4096]{1,0:T(8,128)(2,1)S(1)} %bitcast.2, bf16[4096,256]{1,0:T(8,128)(2,1)S(1)} %copy-done.2, f32[8,128]{1,0:T(8,128)S(1)} %get-tuple-element.99.refs_2_), custom_call_target="tpu_custom_call" | custom-call | tf_op jit(solution)/shard_map/pallas_call | solution.py:67
  7.6 0.2 collective-permute-done.1.refs_1_
  7.9 2.1 %collective-permute-start.2 = (f32[8,128]{1,0:T(8,128)S(1)}, f32[8,128]{1,0:T(8,128)S(1)}, u32[]{:S(2)}, u32[]{:S(2)}) collective-permute-start(f32[8,128]{1,0:T(8,128)S(1)} %get-tuple-element.107.refs_4_), channel_id=1, source_target_pairs={{0,4},{1,5},{2,6},{3,7},{4,0},{5,1},{6,2},{7,3},{8,12},{9,13},{10,... | collective-permute-start | bytes 12296 | tf_op jit(solution)/shard_map/ppermute | solution.py:29
  10.0 1.3 %shard_map.108 = (f32[256,512]{1,0:T(8,128)S(1)}, f32[8,128]{1,0:T(8,128)S(1)}) custom-call(bf16[512,4096]{1,0:T(8,128)(2,1)S(1)} %bitcast.10, bf16[4096,256]{1,0:T(8,128)(2,1)S(1)} %copy-done.3, f32[8,128]{1,0:T(8,128)S(1)} %get-tuple-element.104.refs_2_), custom_call_target="tpu_custom_call" | custom-call | tf_op jit(solution)/shard_map/pallas_call | solution.py:67
  11.3 0.3 collective-permute-done.2.refs_5_
  11.6 0.2 shard_map.109
  11.8 0.5 shard_map.110
  12.3 0.1 collective-permute-start.3
  12.4 0.8 shard_map.111
  13.1 0.6 collective-permute-start.4
  13.7 0.6 collective-permute-done.3.refs_1_
  14.3 0.1 shard_map.112
  14.3 1.1 %shard_map.113 = (f32[8,112,128]{2,1,0:T(8,128)S(1)}, f32[8,152,128]{2,1,0:T(8,128)S(1)}, f32[8,128]{1,0:T(8,128)S(1)}) custom-call(bf16[512,4096]{1,0:T(8,128)(2,1)S(1)} %bitcast.5, bf16[512,4096]{1,0:T(8,128)(2,1)S(1)} %bitcast.13, bf16[256,512]{1,0:T(8,128)(2,1)S(1)} %get-tuple-element.111.refs_2_, bf16[256,512]{1,0:T(8,128)(2,1)S(1)} %get-tuple-element.112.refs_3_, ...), custom_call_target="tpu_custom_call" | custom-call | tf_op jit(solution)/shard_map/pallas_call | solution.py:67
  15.4 0.2 collective-permute-start.5
  15.6 0.1 shard_map.114
  15.7 1.1 %shard_map.115 = (f32[8,152,128]{2,1,0:T(8,128)S(1)}, f32[8,120,128]{2,1,0:T(8,128)S(1)}, f32[8,128]{1,0:T(8,128)S(1)}) custom-call(bf16[512,4096]{1,0:T(8,128)(2,1)S(1)} %bitcast.6, bf16[512,4096]{1,0:T(8,128)(2,1)S(1)} %bitcast.14, bf16[256,512]{1,0:T(8,128)(2,1)S(1)} %get-tuple-element.111.refs_2_, bf16[256,512]{1,0:T(8,128)(2,1)S(1)} %get-tuple-element.112.refs_3_, ...), custom_call_target="tpu_custom_call" | custom-call | tf_op jit(solution)/shard_map/pallas_call | solution.py:67
  16.7 0.4 collective-permute-start.6
  17.2 2.0 %collective-permute-start.8 = (f32[8,128,128]{2,1,0:T(8,128)S(1)}, f32[8,128,128]{2,1,0:T(8,128)S(1)}, u32[]{:S(2)}, u32[]{:S(2)}) collective-permute-start(f32[8,128,128]{2,1,0:T(8,128)S(1)} %get-tuple-element.134), channel_id=1, source_target_pairs={{0,4},{1,3},{2,6},{3,1},{4,0},{5,7},{6,2},{7,5},{8,12},{9,11},{10,... | collective-permute-start | bytes 1572872 | tf_op jit(solution)/shard_map/ppermute | solution.py:29
  19.2 0.1 shard_map.116
  19.3 0.5 shard_map.117
  19.7 0.1 shard_map.118
  19.8 1.7 %shard_map.119 = (f32[8,128,128]{2,1,0:T(8,128)S(1)}, f32[8,112,128]{2,1,0:T(8,128)S(1)}, f32[8,152,128]{2,1,0:T(8,128)S(1)}, f32[8,120,128]{2,1,0:T(8,128)S(1)}, f32[8,128]{1,0:T(8,128)S(1)}) custom-call(bf16[512,4096]{1,0:T(8,128)(2,1)S(1)} %bitcast.8, bf16[512,4096]{1,0:T(8,128)(2,1)S(1)} %bitcast.16, bf16[256,512]{1,0:T(8,128)(2,1)S(1)} %get-tuple-element.111.refs_2_, ...), custom_call_target="tpu_custom_call" | custom-call | tf_op jit(solution)/shard_map/pallas_call | solution.py:67
  21.5 0.1 collective-permute-start.7
  21.6 1.5 %collective-permute-start.15 = (f32[8,112,128]{2,1,0:T(8,128)S(1)}, f32[8,112,128]{2,1,0:T(8,128)S(1)}, u32[]{:S(2)}, u32[]{:S(2)}) collective-permute-start(f32[8,112,128]{2,1,0:T(8,128)S(1)} %get-tuple-element.146), channel_id=1, source_target_pairs={{0,2},{1,5},{2,0},{3,7},{4,6},{5,1},{6,4},{7,3},{8,10},{9,13},{10,... | collective-permute-start | bytes 1376264 | tf_op jit(solution)/shard_map/ppermute | solution.py:29
  23.1 1.6 %collective-permute-start.11 = (f32[8,152,128]{2,1,0:T(8,128)S(1)}, f32[8,152,128]{2,1,0:T(8,128)S(1)}, u32[]{:S(2)}, u32[]{:S(2)}) collective-permute-start(f32[8,152,128]{2,1,0:T(8,128)S(1)} %get-tuple-element.140), channel_id=1, source_target_pairs={{0,8},{1,9},{2,10},{3,11},{4,12},{5,13},{6,14},{7,15},{8,0},{9,1},... | collective-permute-start | bytes 1867784 | tf_op jit(solution)/shard_map/ppermute | solution.py:29
  24.7 6.0 %collective-permute-done.15.refs_2_ = f32[8,112,128]{2,1,0:T(8,128)S(1)} collective-permute-done((f32[8,112,128]{2,1,0:T(8,128)S(1)}, f32[8,112,128]{2,1,0:T(8,128)S(1)}, u32[]{:S(2)}, u32[]{:S(2)}) %collective-permute-start.15) | collective-permute-done | bytes 458784 | tf_op jit(solution)/shard_map/ppermute | solution.py:29
  30.7 1.7 %collective-permute-start.13 = (f32[8,120,128]{2,1,0:T(8,128)S(1)}, f32[8,120,128]{2,1,0:T(8,128)S(1)}, u32[]{:S(2)}, u32[]{:S(2)}) collective-permute-start(f32[8,120,128]{2,1,0:T(8,128)S(1)} %get-tuple-element.143), channel_id=1, source_target_pairs={{0,2},{1,5},{2,0},{3,7},{4,6},{5,1},{6,4},{7,3},{8,10},{9,13},{10,... | collective-permute-start | bytes 1474568 | tf_op jit(solution)/shard_map/ppermute | solution.py:29
  32.4 0.7 collective-permute-start.12
  33.1 0.1 collective-permute-start.14
  33.2 1.6 %shard_map.120 = (f32[8,128,128]{2,1,0:T(8,128)S(1)}, f32[8,112,128]{2,1,0:T(8,128)S(1)}, f32[8,152,128]{2,1,0:T(8,128)S(1)}, f32[8,120,128]{2,1,0:T(8,128)S(1)}, f32[8,128]{1,0:T(8,128)S(1)}) custom-call(bf16[512,4096]{1,0:T(8,128)(2,1)S(1)} %bitcast.9, bf16[512,4096]{1,0:T(8,128)(2,1)S(1)} %bitcast.17, bf16[256,512]{1,0:T(8,128)(2,1)S(1)} %get-tuple-element.111.refs_2_, ...), custom_call_target="tpu_custom_call" | custom-call | tf_op jit(solution)/shard_map/pallas_call | solution.py:67
  34.8 0.1 shard_map.121
  35.0 0.3 collective-permute-done.14.refs_1_
  35.3 0.1 shard_map.122
  35.4 4.1 %collective-permute-done.13.refs_2_ = f32[8,120,128]{2,1,0:T(8,128)S(1)} collective-permute-done((f32[8,120,128]{2,1,0:T(8,128)S(1)}, f32[8,120,128]{2,1,0:T(8,128)S(1)}, u32[]{:S(2)}, u32[]{:S(2)}) %collective-permute-start.13) | collective-permute-done | bytes 491552 | tf_op jit(solution)/shard_map/ppermute | solution.py:29
  39.5 0.1 shard_map.123
  39.6 0.1 shard_map.124
  39.7 1.8 %collective-permute-start.17 = (f32[4,152,128]{2,1,0:T(8,128)S(1)}, f32[4,152,128]{2,1,0:T(8,128)S(1)}, u32[]{:S(2)}, u32[]{:S(2)}) collective-permute-start(f32[4,152,128]{2,1,0:T(8,128)S(1)} %get-tuple-element.154), channel_id=1, source_target_pairs={{0,4},{1,3},{2,6},{3,1},{4,0},{5,7},{6,2},{7,5},{8,12},{9,11},{10,... | collective-permute-start | bytes 933896 | tf_op jit(solution)/shard_map/ppermute | solution.py:29
  41.6 1.5 %collective-permute-start.9 = (f32[4,128,128]{2,1,0:T(8,128)S(1)}, f32[4,128,128]{2,1,0:T(8,128)S(1)}, u32[]{:S(2)}, u32[]{:S(2)}) collective-permute-start(f32[4,128,128]{2,1,0:T(8,128)S(1)} %get-tuple-element.137), channel_id=1, source_target_pairs={{0,2},{1,5},{2,0},{3,7},{4,6},{5,1},{6,4},{7,3},{8,10},{9,13},{10,... | collective-permute-start | bytes 786440 | tf_op jit(solution)/shard_map/ppermute | solution.py:29
  43.1 0.5 collective-permute-start.18
  43.6 1.6 %collective-permute-start.19 = (f32[4,112,128]{2,1,0:T(8,128)S(1)}, f32[4,112,128]{2,1,0:T(8,128)S(1)}, u32[]{:S(2)}, u32[]{:S(2)}) collective-permute-start(f32[4,112,128]{2,1,0:T(8,128)S(1)} %get-tuple-element.158), channel_id=1, source_target_pairs={{0,8},{1,9},{2,10},{3,11},{4,12},{5,13},{6,14},{7,15},{8,0},{9,1},... | collective-permute-start | bytes 688136 | tf_op jit(solution)/shard_map/ppermute | solution.py:29
  45.1 5.6 %collective-permute-done.9.refs_1_ = f32[4,128,128]{2,1,0:T(8,128)S(1)} collective-permute-done((f32[4,128,128]{2,1,0:T(8,128)S(1)}, f32[4,128,128]{2,1,0:T(8,128)S(1)}, u32[]{:S(2)}, u32[]{:S(2)}) %collective-permute-start.9) | collective-permute-done | bytes 262176 | tf_op jit(solution)/shard_map/ppermute | solution.py:29
  50.8 1.3 %collective-permute-done.18.refs_1_ = f32[4,120,128]{2,1,0:T(8,128)S(1)} collective-permute-done((f32[4,120,128]{2,1,0:T(8,128)S(1)}, f32[4,120,128]{2,1,0:T(8,128)S(1)}, u32[]{:S(2)}, u32[]{:S(2)}) %collective-permute-start.18) | collective-permute-done | bytes 245792 | tf_op jit(solution)/shard_map/ppermute | solution.py:29
  52.2 1.0 %collective-permute-start.22 = (f32[2,152,128]{2,1,0:T(8,128)S(1)}, f32[2,152,128]{2,1,0:T(8,128)S(1)}, u32[]{:S(2)}, u32[]{:S(2)}) collective-permute-start(f32[2,152,128]{2,1,0:T(8,128)S(1)} %get-tuple-element.169), channel_id=1, source_target_pairs={{0,2},{1,5},{2,0},{3,7},{4,6},{5,1},{6,4},{7,3},{8,10},{9,13},{10,... | collective-permute-start | bytes 466952 | tf_op jit(solution)/shard_map/ppermute | solution.py:29
  53.2 1.8 %collective-permute-start.16 = (f32[2,128,128]{2,1,0:T(8,128)S(1)}, f32[2,128,128]{2,1,0:T(8,128)S(1)}, u32[]{:S(2)}, u32[]{:S(2)}) collective-permute-start(f32[2,128,128]{2,1,0:T(8,128)S(1)} %get-tuple-element.152), channel_id=1, source_target_pairs={{0,8},{1,9},{2,10},{3,11},{4,12},{5,13},{6,14},{7,15},{8,0},{9,1},... | collective-permute-start | bytes 393224 | tf_op jit(solution)/shard_map/ppermute | solution.py:29
  55.0 0.3 collective-permute-start.21
  55.3 2.8 %collective-permute-start.20 = (f32[2,112,128]{2,1,0:T(8,128)S(1)}, f32[2,112,128]{2,1,0:T(8,128)S(1)}, u32[]{:S(2)}, u32[]{:S(2)}) collective-permute-start(f32[2,112,128]{2,1,0:T(8,128)S(1)} %get-tuple-element.165), channel_id=1, source_target_pairs={{0,16},{1,17},{2,18},{3,19},{4,20},{5,21},{6,22},{7,23},{8,24},{9,... | collective-permute-start | bytes 344072 | tf_op jit(solution)/shard_map/ppermute | solution.py:29
  58.0 4.8 %collective-permute-done.16.refs_1_ = f32[2,128,128]{2,1,0:T(8,128)S(1)} collective-permute-done((f32[2,128,128]{2,1,0:T(8,128)S(1)}, f32[2,128,128]{2,1,0:T(8,128)S(1)}, u32[]{:S(2)}, u32[]{:S(2)}) %collective-permute-start.16) | collective-permute-done | bytes 131104 | tf_op jit(solution)/shard_map/ppermute | solution.py:29
  63.0 0.8 collective-permute-start.25
  63.7 2.2 %collective-permute-start.23 = (f32[1,128,128]{2,1,0:T(8,128)S(1)}, f32[1,128,128]{2,1,0:T(8,128)S(1)}, u32[]{:S(2)}, u32[]{:S(2)}) collective-permute-start(f32[1,128,128]{2,1,0:T(8,128)S(1)} %get-tuple-element.176), channel_id=1, source_target_pairs={{0,16},{1,17},{2,18},{3,19},{4,20},{5,21},{6,22},{7,23},{8,24},{9,... | collective-permute-start | bytes 196616 | tf_op jit(solution)/shard_map/ppermute | solution.py:29
  66.0 0.8 collective-permute-start.26
  66.8 2.6 %collective-permute-start.24 = (f32[1,112,128]{2,1,0:T(8,128)S(1)}, f32[1,112,128]{2,1,0:T(8,128)S(1)}, u32[]{:S(2)}, u32[]{:S(2)}) collective-permute-start(f32[1,112,128]{2,1,0:T(8,128)S(1)} %get-tuple-element.177), channel_id=1, source_target_pairs={{0,4},{1,3},{2,6},{3,1},{4,0},{5,7},{6,2},{7,5},{8,12},{9,11},{10,... | collective-permute-start | bytes 172040 | tf_op jit(solution)/shard_map/ppermute | solution.py:29
  69.4 2.8 %collective-permute-done.23.refs_4_ = f32[1,128,128]{2,1,0:T(8,128)S(1)} collective-permute-done((f32[1,128,128]{2,1,0:T(8,128)S(1)}, f32[1,128,128]{2,1,0:T(8,128)S(1)}, u32[]{:S(2)}, u32[]{:S(2)}) %collective-permute-start.23) | collective-permute-done | bytes 65568 | tf_op jit(solution)/shard_map/ppermute | solution.py:29
  72.2 0.7 collective-permute-done.26.refs_7_
  72.8 0.7 shard_map.133
  73.5 5.2 %all-to-all-start = ((f32[32,1,128]{2,1,0:T(1,128)}), f32[32,1,128]{2,1,0:T(1,128)S(1)}, u32[]{:S(2)}, u32[]{:S(2)}) async-start(f32[32,1,128]{2,1,0:T(1,128)} %get-tuple-element.183), calls=%async_computation | async-start | bytes 32768 | tf_op jit(solution)/shard_map/all_to_all | solution.py:329
  78.7 0.6 copy.11
  79.3 6.5 %all-to-all-done.refs_2_ = f32[32,1,128]{2,1,0:T(1,128)S(1)} async-done(((f32[32,1,128]{2,1,0:T(1,128)}), f32[32,1,128]{2,1,0:T(1,128)S(1)}, u32[]{:S(2)}, u32[]{:S(2)}) %all-to-all-start) | async-done | bytes 16416 | tf_op jit(solution)/shard_map/all_to_all | solution.py:329
  85.8 0.9 %shard_map.134 = (f32[128,256]{1,0:T(8,128)}, f32[128,256]{1,0:T(8,128)}, f32[8,128]{1,0:T(8,128)}) custom-call(f32[256,128]{1,0:T(8,128)S(1)} %get-tuple-element.181.refs_0_, f32[256,128]{1,0:T(8,128)S(1)} %get-tuple-element.182.refs_1_, f32[32,1,128]{2,1,0:T(1,128)S(1)} %all-to-all-done.refs_2_, f32[8,128]{1,0:T(8,128)S(1)} %get-tuple-element.184.refs_3_), custom_call_target="tpu_custom_call" | custom-call | tf_op jit(solution)/shard_map/pallas_call | solution.py:67
  (40 shorter events, 0.3 us)
Async XLA Ops:
  1.3 0.7 copy-start.6
  2.1 1.3 %collective-permute-start = (f32[8,128]{1,0:T(8,128)S(1)}, f32[8,128]{1,0:T(8,128)S(1)}, u32[]{:S(2)}, u32[]{:S(2)}) collective-permute-start(f32[8,128]{1,0:T(8,128)S(1)} %get-tuple-element.95.refs_0_), channel_id=1, source_target_pairs={{0,1},{1,0},{2,3},{3,2},{4,5},{5,4},{6,7},{7,6},{8,9},{9,8},{10,11... | collective-permute-start | bytes 12296 | tf_op jit(solution)/shard_map/ppermute | solution.py:29
  2.6 3.7 %copy-start = (bf16[1,512,4096]{2,1,0:T(8,128)(2,1)S(1)}, bf16[1,512,4096]{2,1,0:T(8,128)(2,1)}, u32[]{:S(2)}) copy-start(bf16[1,512,4096]{2,1,0:T(8,128)(2,1)} %param.8) | copy-start | bytes 12582916
  2.6 3.7 %copy-start.2 = (bf16[4096,256]{1,0:T(8,128)(2,1)S(1)}, bf16[4096,256]{1,0:T(8,128)(2,1)}, u32[]{:S(2)}) copy-start(bf16[4096,256]{1,0:T(8,128)(2,1)} %refs_1_.4) | copy-start | bytes 6291460
  2.8 7.2 %copy-start.1 = (bf16[1,512,4096]{2,1,0:T(8,128)(2,1)S(1)}, bf16[1,512,4096]{2,1,0:T(8,128)(2,1)}, u32[]{:S(2)}) copy-start(bf16[1,512,4096]{2,1,0:T(8,128)(2,1)} %param.9) | copy-start | bytes 12582916
  2.8 7.2 %copy-start.3 = (bf16[4096,256]{1,0:T(8,128)(2,1)S(1)}, bf16[4096,256]{1,0:T(8,128)(2,1)}, u32[]{:S(2)}) copy-start(bf16[4096,256]{1,0:T(8,128)(2,1)} %refs_1_.5) | copy-start | bytes 6291460
  3.4 4.5 %collective-permute-start.1 = (f32[8,128]{1,0:T(8,128)S(1)}, f32[8,128]{1,0:T(8,128)S(1)}, u32[]{:S(2)}, u32[]{:S(2)}) collective-permute-start(f32[8,128]{1,0:T(8,128)S(1)} %get-tuple-element.101.refs_0_), channel_id=1, source_target_pairs={{0,2},{1,3},{2,0},{3,1},{4,6},{5,7},{6,4},{7,5},{8,10},{9,11},{10,... | collective-permute-start | bytes 12296 | tf_op jit(solution)/shard_map/ppermute | solution.py:29
  7.6 4.0 %copy-start.4 = (f32[1,512]{1,0:T(1,128)S(1)}, f32[1,512]{1,0:T(1,128)}, u32[]{:S(2)}) copy-start(f32[1,512]{1,0:T(1,128)} %refs_7_.1) | copy-start | bytes 6148
  7.6 4.0 %copy-start.5 = (f32[1,512]{1,0:T(1,128)S(1)}, f32[1,512]{1,0:T(1,128)}, u32[]{:S(2)}) copy-start(f32[1,512]{1,0:T(1,128)} %refs_8_.1) | copy-start | bytes 6148
  7.9 3.7 %collective-permute-start.2 = (f32[8,128]{1,0:T(8,128)S(1)}, f32[8,128]{1,0:T(8,128)S(1)}, u32[]{:S(2)}, u32[]{:S(2)}) collective-permute-start(f32[8,128]{1,0:T(8,128)S(1)} %get-tuple-element.107.refs_4_), channel_id=1, source_target_pairs={{0,4},{1,5},{2,6},{3,7},{4,0},{5,1},{6,2},{7,3},{8,12},{9,13},{10,... | collective-permute-start | bytes 12296 | tf_op jit(solution)/shard_map/ppermute | solution.py:29
  12.3 2.0 %collective-permute-start.3 = (f32[8,128,128]{2,1,0:T(8,128)S(1)}, f32[8,128,128]{2,1,0:T(8,128)S(1)}, u32[]{:S(2)}, u32[]{:S(2)}) collective-permute-start(f32[8,128,128]{2,1,0:T(8,128)S(1)} %get-tuple-element.116), channel_id=1, source_target_pairs={{0,1},{1,0},{2,3},{3,2},{4,5},{5,4},{6,7},{7,6},{8,9},{9,8},{10,11... | collective-permute-start | bytes 1572872 | tf_op jit(solution)/shard_map/ppermute | solution.py:29
  13.1 2.5 %collective-permute-start.4 = (f32[8,112,128]{2,1,0:T(8,128)S(1)}, f32[8,112,128]{2,1,0:T(8,128)S(1)}, u32[]{:S(2)}, u32[]{:S(2)}) collective-permute-start(f32[8,112,128]{2,1,0:T(8,128)S(1)} %get-tuple-element.120), channel_id=1, source_target_pairs={{0,1},{1,0},{2,3},{3,2},{4,5},{5,4},{6,7},{7,6},{8,9},{9,8},{10,11... | collective-permute-start | bytes 1376264 | tf_op jit(solution)/shard_map/ppermute | solution.py:29
  15.4 3.8 %collective-permute-start.5 = (f32[8,152,128]{2,1,0:T(8,128)S(1)}, f32[8,152,128]{2,1,0:T(8,128)S(1)}, u32[]{:S(2)}, u32[]{:S(2)}) collective-permute-start(f32[8,152,128]{2,1,0:T(8,128)S(1)} %get-tuple-element.124), channel_id=1, source_target_pairs={{0,1},{1,0},{2,3},{3,2},{4,5},{5,4},{6,7},{7,6},{8,9},{9,8},{10,11... | collective-permute-start | bytes 1867784 | tf_op jit(solution)/shard_map/ppermute | solution.py:29
  16.7 3.0 %collective-permute-start.6 = (f32[8,120,128]{2,1,0:T(8,128)S(1)}, f32[8,120,128]{2,1,0:T(8,128)S(1)}, u32[]{:S(2)}, u32[]{:S(2)}) collective-permute-start(f32[8,120,128]{2,1,0:T(8,128)S(1)} %get-tuple-element.128), channel_id=1, source_target_pairs={{0,1},{1,0},{2,3},{3,2},{4,5},{5,4},{6,7},{7,6},{8,9},{9,8},{10,11... | collective-permute-start | bytes 1474568 | tf_op jit(solution)/shard_map/ppermute | solution.py:29
  17.2 15.2 %collective-permute-start.8 = (f32[8,128,128]{2,1,0:T(8,128)S(1)}, f32[8,128,128]{2,1,0:T(8,128)S(1)}, u32[]{:S(2)}, u32[]{:S(2)}) collective-permute-start(f32[8,128,128]{2,1,0:T(8,128)S(1)} %get-tuple-element.134), channel_id=1, source_target_pairs={{0,4},{1,3},{2,6},{3,1},{4,0},{5,7},{6,2},{7,5},{8,12},{9,11},{10,... | collective-permute-start | bytes 1572872 | tf_op jit(solution)/shard_map/ppermute | solution.py:29
  21.5 11.6 %collective-permute-start.7 = (f32[8,128,128]{2,1,0:T(8,128)S(1)}, f32[8,128,128]{2,1,0:T(8,128)S(1)}, u32[]{:S(2)}, u32[]{:S(2)}) collective-permute-start(f32[8,128,128]{2,1,0:T(8,128)S(1)} %get-tuple-element.133), channel_id=1, source_target_pairs={{0,1},{1,0},{2,3},{3,2},{4,5},{5,4},{6,7},{7,6},{8,9},{9,8},{10,11... | collective-permute-start | bytes 1572872 | tf_op jit(solution)/shard_map/ppermute | solution.py:29
  21.6 9.1 %collective-permute-start.15 = (f32[8,112,128]{2,1,0:T(8,128)S(1)}, f32[8,112,128]{2,1,0:T(8,128)S(1)}, u32[]{:S(2)}, u32[]{:S(2)}) collective-permute-start(f32[8,112,128]{2,1,0:T(8,128)S(1)} %get-tuple-element.146), channel_id=1, source_target_pairs={{0,2},{1,5},{2,0},{3,7},{4,6},{5,1},{6,4},{7,3},{8,10},{9,13},{10,... | collective-permute-start | bytes 1376264 | tf_op jit(solution)/shard_map/ppermute | solution.py:29
  23.1 16.5 %collective-permute-start.11 = (f32[8,152,128]{2,1,0:T(8,128)S(1)}, f32[8,152,128]{2,1,0:T(8,128)S(1)}, u32[]{:S(2)}, u32[]{:S(2)}) collective-permute-start(f32[8,152,128]{2,1,0:T(8,128)S(1)} %get-tuple-element.140), channel_id=1, source_target_pairs={{0,8},{1,9},{2,10},{3,11},{4,12},{5,13},{6,14},{7,15},{8,0},{9,1},... | collective-permute-start | bytes 1867784 | tf_op jit(solution)/shard_map/ppermute | solution.py:29
  24.7 14.9 %collective-permute-start.10 = (f32[8,152,128]{2,1,0:T(8,128)S(1)}, f32[8,152,128]{2,1,0:T(8,128)S(1)}, u32[]{:S(2)}, u32[]{:S(2)}) collective-permute-start(f32[8,152,128]{2,1,0:T(8,128)S(1)} %get-tuple-element.139), channel_id=1, source_target_pairs={{0,1},{1,0},{2,3},{3,2},{4,5},{5,4},{6,7},{7,6},{8,9},{9,8},{10,11... | collective-permute-start | bytes 1867784 | tf_op jit(solution)/shard_map/ppermute | solution.py:29
  30.7 8.8 %collective-permute-start.13 = (f32[8,120,128]{2,1,0:T(8,128)S(1)}, f32[8,120,128]{2,1,0:T(8,128)S(1)}, u32[]{:S(2)}, u32[]{:S(2)}) collective-permute-start(f32[8,120,128]{2,1,0:T(8,128)S(1)} %get-tuple-element.143), channel_id=1, source_target_pairs={{0,2},{1,5},{2,0},{3,7},{4,6},{5,1},{6,4},{7,3},{8,10},{9,13},{10,... | collective-permute-start | bytes 1474568 | tf_op jit(solution)/shard_map/ppermute | solution.py:29
  32.4 7.1 %collective-permute-start.12 = (f32[8,120,128]{2,1,0:T(8,128)S(1)}, f32[8,120,128]{2,1,0:T(8,128)S(1)}, u32[]{:S(2)}, u32[]{:S(2)}) collective-permute-start(f32[8,120,128]{2,1,0:T(8,128)S(1)} %get-tuple-element.142), channel_id=1, source_target_pairs={{0,1},{1,0},{2,3},{3,2},{4,5},{5,4},{6,7},{7,6},{8,9},{9,8},{10,11... | collective-permute-start | bytes 1474568 | tf_op jit(solution)/shard_map/ppermute | solution.py:29
  33.1 2.1 %collective-permute-start.14 = (f32[8,112,128]{2,1,0:T(8,128)S(1)}, f32[8,112,128]{2,1,0:T(8,128)S(1)}, u32[]{:S(2)}, u32[]{:S(2)}) collective-permute-start(f32[8,112,128]{2,1,0:T(8,128)S(1)} %get-tuple-element.145), channel_id=1, source_target_pairs={{0,1},{1,0},{2,3},{3,2},{4,5},{5,4},{6,7},{7,6},{8,9},{9,8},{10,11... | collective-permute-start | bytes 1376264 | tf_op jit(solution)/shard_map/ppermute | solution.py:29
  39.7 12.4 %collective-permute-start.17 = (f32[4,152,128]{2,1,0:T(8,128)S(1)}, f32[4,152,128]{2,1,0:T(8,128)S(1)}, u32[]{:S(2)}, u32[]{:S(2)}) collective-permute-start(f32[4,152,128]{2,1,0:T(8,128)S(1)} %get-tuple-element.154), channel_id=1, source_target_pairs={{0,4},{1,3},{2,6},{3,1},{4,0},{5,7},{6,2},{7,5},{8,12},{9,11},{10,... | collective-permute-start | bytes 933896 | tf_op jit(solution)/shard_map/ppermute | solution.py:29
  41.6 9.2 %collective-permute-start.9 = (f32[4,128,128]{2,1,0:T(8,128)S(1)}, f32[4,128,128]{2,1,0:T(8,128)S(1)}, u32[]{:S(2)}, u32[]{:S(2)}) collective-permute-start(f32[4,128,128]{2,1,0:T(8,128)S(1)} %get-tuple-element.137), channel_id=1, source_target_pairs={{0,2},{1,5},{2,0},{3,7},{4,6},{5,1},{6,4},{7,3},{8,10},{9,13},{10,... | collective-permute-start | bytes 786440 | tf_op jit(solution)/shard_map/ppermute | solution.py:29
  43.1 9.1 %collective-permute-start.18 = (f32[4,120,128]{2,1,0:T(8,128)S(1)}, f32[4,120,128]{2,1,0:T(8,128)S(1)}, u32[]{:S(2)}, u32[]{:S(2)}) collective-permute-start(f32[4,120,128]{2,1,0:T(8,128)S(1)} %get-tuple-element.156), channel_id=1, source_target_pairs={{0,4},{1,3},{2,6},{3,1},{4,0},{5,7},{6,2},{7,5},{8,12},{9,11},{10,... | collective-permute-start | bytes 737288 | tf_op jit(solution)/shard_map/ppermute | solution.py:29
  43.6 7.2 %collective-permute-start.19 = (f32[4,112,128]{2,1,0:T(8,128)S(1)}, f32[4,112,128]{2,1,0:T(8,128)S(1)}, u32[]{:S(2)}, u32[]{:S(2)}) collective-permute-start(f32[4,112,128]{2,1,0:T(8,128)S(1)} %get-tuple-element.158), channel_id=1, source_target_pairs={{0,8},{1,9},{2,10},{3,11},{4,12},{5,13},{6,14},{7,15},{8,0},{9,1},... | collective-permute-start | bytes 688136 | tf_op jit(solution)/shard_map/ppermute | solution.py:29
  52.2 10.7 %collective-permute-start.22 = (f32[2,152,128]{2,1,0:T(8,128)S(1)}, f32[2,152,128]{2,1,0:T(8,128)S(1)}, u32[]{:S(2)}, u32[]{:S(2)}) collective-permute-start(f32[2,152,128]{2,1,0:T(8,128)S(1)} %get-tuple-element.169), channel_id=1, source_target_pairs={{0,2},{1,5},{2,0},{3,7},{4,6},{5,1},{6,4},{7,3},{8,10},{9,13},{10,... | collective-permute-start | bytes 466952 | tf_op jit(solution)/shard_map/ppermute | solution.py:29
  53.2 9.7 %collective-permute-start.16 = (f32[2,128,128]{2,1,0:T(8,128)S(1)}, f32[2,128,128]{2,1,0:T(8,128)S(1)}, u32[]{:S(2)}, u32[]{:S(2)}) collective-permute-start(f32[2,128,128]{2,1,0:T(8,128)S(1)} %get-tuple-element.152), channel_id=1, source_target_pairs={{0,8},{1,9},{2,10},{3,11},{4,12},{5,13},{6,14},{7,15},{8,0},{9,1},... | collective-permute-start | bytes 393224 | tf_op jit(solution)/shard_map/ppermute | solution.py:29
  55.0 10.9 %collective-permute-start.21 = (f32[2,120,128]{2,1,0:T(8,128)S(1)}, f32[2,120,128]{2,1,0:T(8,128)S(1)}, u32[]{:S(2)}, u32[]{:S(2)}) collective-permute-start(f32[2,120,128]{2,1,0:T(8,128)S(1)} %get-tuple-element.167), channel_id=1, source_target_pairs={{0,8},{1,9},{2,10},{3,11},{4,12},{5,13},{6,14},{7,15},{8,0},{9,1},... | collective-permute-start | bytes 368648 | tf_op jit(solution)/shard_map/ppermute | solution.py:29
  55.3 11.5 %collective-permute-start.20 = (f32[2,112,128]{2,1,0:T(8,128)S(1)}, f32[2,112,128]{2,1,0:T(8,128)S(1)}, u32[]{:S(2)}, u32[]{:S(2)}) collective-permute-start(f32[2,112,128]{2,1,0:T(8,128)S(1)} %get-tuple-element.165), channel_id=1, source_target_pairs={{0,16},{1,17},{2,18},{3,19},{4,20},{5,21},{6,22},{7,23},{8,24},{9,... | collective-permute-start | bytes 344072 | tf_op jit(solution)/shard_map/ppermute | solution.py:29
  63.0 9.9 %collective-permute-start.25 = (f32[1,152,128]{2,1,0:T(8,128)S(1)}, f32[1,152,128]{2,1,0:T(8,128)S(1)}, u32[]{:S(2)}, u32[]{:S(2)}) collective-permute-start(f32[1,152,128]{2,1,0:T(8,128)S(1)} %get-tuple-element.178), channel_id=1, source_target_pairs={{0,16},{1,17},{2,18},{3,19},{4,20},{5,21},{6,22},{7,23},{8,24},{9,... | collective-permute-start | bytes 233480 | tf_op jit(solution)/shard_map/ppermute | solution.py:29
  63.7 8.4 %collective-permute-start.23 = (f32[1,128,128]{2,1,0:T(8,128)S(1)}, f32[1,128,128]{2,1,0:T(8,128)S(1)}, u32[]{:S(2)}, u32[]{:S(2)}) collective-permute-start(f32[1,128,128]{2,1,0:T(8,128)S(1)} %get-tuple-element.176), channel_id=1, source_target_pairs={{0,16},{1,17},{2,18},{3,19},{4,20},{5,21},{6,22},{7,23},{8,24},{9,... | collective-permute-start | bytes 196616 | tf_op jit(solution)/shard_map/ppermute | solution.py:29
  66.0 6.9 %collective-permute-start.26 = (f32[1,120,128]{2,1,0:T(8,128)S(1)}, f32[1,120,128]{2,1,0:T(8,128)S(1)}, u32[]{:S(2)}, u32[]{:S(2)}) collective-permute-start(f32[1,120,128]{2,1,0:T(8,128)S(1)} %get-tuple-element.179), channel_id=1, source_target_pairs={{0,16},{1,17},{2,18},{3,19},{4,20},{5,21},{6,22},{7,23},{8,24},{9,... | collective-permute-start | bytes 184328 | tf_op jit(solution)/shard_map/ppermute | solution.py:29
  66.8 5.4 %collective-permute-start.24 = (f32[1,112,128]{2,1,0:T(8,128)S(1)}, f32[1,112,128]{2,1,0:T(8,128)S(1)}, u32[]{:S(2)}, u32[]{:S(2)}) collective-permute-start(f32[1,112,128]{2,1,0:T(8,128)S(1)} %get-tuple-element.177), channel_id=1, source_target_pairs={{0,4},{1,3},{2,6},{3,1},{4,0},{5,7},{6,2},{7,5},{8,12},{9,11},{10,... | collective-permute-start | bytes 172040 | tf_op jit(solution)/shard_map/ppermute | solution.py:29
  73.5 12.3 %all-to-all-start = ((f32[32,1,128]{2,1,0:T(1,128)}), f32[32,1,128]{2,1,0:T(1,128)S(1)}, u32[]{:S(2)}, u32[]{:S(2)}) async-start(f32[32,1,128]{2,1,0:T(1,128)} %get-tuple-element.183), calls=%async_computation | async-start | bytes 32768 | tf_op jit(solution)/shard_map/all_to_all | solution.py:329

commit v3 on v2

--- a/solution.py
+++ b/solution.py
@@ -1,4 +1,5 @@
 import functools
+import itertools
 import math
 
 import jax
@@ -16,7 +17,7 @@
 KERNEL_VMEM = 8 * 1024 * 1024
 F32 = jnp.float32
 
-PARTS = (("yxzw", "xyzw", 16), ("xzwy", "yzwx", 14), ("zyxw", "zxyw", 19), ("xyzw", "yxzw", 15))
+PARTS = (("yxzw", "xyzw", 17), ("xzwy", "yzwx", 13), ("zyxw", "zxyw", 19), ("xyzw", "yxzw", 15))
 TURNS = (0, 1, 3, 2, 0, 1, 3, 2, 0, 2, 3, 1)
 
 SMEM = pl.BlockSpec(memory_space=pltpu.SMEM)
@@ -204,8 +205,13 @@
 def clip_body(down, up, squares, grad_down, grad_up, *, clip_norm):
     norm = jnp.sqrt(jnp.sum(jnp.sum(squares[...], axis=0), axis=1, keepdims=True))
     factor = clip_norm / jnp.maximum(norm, clip_norm)
-    grad_down[...] = (down[...] * factor).T
-    grad_up[...] = (up[...] * factor).T
+    grad_down[...] = down[...] * factor
+    grad_up[...] = up[...] * factor
+
+
+def turn_body(down, up, down_rows, up_rows):
+    down_rows[...] = down[...].T
+    up_rows[...] = up[...].T
 
 
 def tiles_of(order, fixed):
@@ -217,6 +223,15 @@
 
 def log2(n):
     return n.bit_length() - 1
+
+
+def laying():
+    n = len(PARTS)
+    for size in range(1, n):
+        for some in itertools.combinations(range(n), size):
+            if sum(PARTS[i][2] for i in some) == 32:
+                return [*some, *[i for i in range(n) if i not in some]]
+    return list(range(n))
 
 
 def script(halvings):
@@ -285,15 +300,15 @@
     core, plane = bits[0], bits[1:]
     zs = [ns << j for j in range(log2(nb))]
     masks = {"x": plane[: len(plane) // 2], "y": plane[len(plane) // 2 :], "z": zs[:-1], "w": zs[-1:]}
-    orders, pieces, at = [], [], 0
-    for even, odd, share in PARTS:
-        orders.append([[m for axis in axes for m in masks[axis]] for axes in (even, odd)])
-        end = at + 2 * rank * share // 64
-        pieces.append([
+    orders = [[[m for axis in axes for m in masks[axis]] for axes in part[:2]] for part in PARTS]
+    pieces, at, laid = [None] * len(PARTS), 0, laying()
+    for i in laid:
+        end = at + 2 * rank * PARTS[i][2] // 64
+        pieces[i] = [
             (side, max(at - side * rank, 0), min(end, rank * (side + 1)) - max(at, rank * side))
             for side in (0, 1)
             if min(end, rank * (side + 1)) > max(at, rank * side)
-        ])
+        ]
         at = end
     n = len(PARTS)
     sends = [(list(zip(*[tiles_of(o[1:], o[0]) for o in orders[i]])), pieces[i]) for i in range(n)]
@@ -324,9 +339,10 @@
 
     down, up, squares = line.call(
         functools.partial(total_body, n=n, rank=rank),
-        [((rank, LANES), F32), ((rank, LANES), F32), ((count, 1, LANES), F32)], (*[k[0] for k in kept], *sent),
+        [((rank, LANES), F32), ((rank, LANES), F32), ((count, 1, LANES), F32)], (*[kept[i][0] for i in laid], *[sent[i] for i in laid]),
     )
     squares = lax.all_to_all(squares, AXES, 0, 0, tiled=True)
+    down, up = line.call(turn_body, [((LANES, rank), F32)] * 2, (down, up))
     clip_norm = 0.5 * math.sqrt(2.0 * width * rank)
     grad_down, grad_up = line.call(
         functools.partial(clip_body, clip_norm=clip_norm), [((LANES, rank), F32)] * 2, (down, up, squares), in_vmem=False

time: 86.9 us -> 85.6 us (0.985)
  starting transfers between devices: 37.3 us -> 34.1 us
  waiting for transfers between devices: 33.8 us -> 36.7 us
  Pallas kernels: 12.8 us -> 11.8 us
    ppermute x27, waiting for transfers between devices: 27.3 us -> 30.3 us  [swap(): lax.ppermute(x, AXES, [(i, i ^ (odd if i & 1 else even)) for i in range(c...]
    ppermute x27, starting transfers between devices: 32.1 us -> 30.1 us  [swap(): lax.ppermute(x, AXES, [(i, i ^ (odd if i & 1 else even)) for i in range(c...]
    all_to_all x1, starting transfers between devices: 5.19 us -> 4.06 us  [in_blocks(): squares = lax.all_to_all(squares, AXES, 0, 0, tiled=True)]
    pallas_call x32 -> x33, Pallas kernels: 12.8 us -> 11.8 us  [call(): *got, self.token = kernel(*scalars, *from_hbm, *ins)]
  transfers between devices with their start and end apart: 28 -> 28, of which waited for: 13 -> 13; matrix products, arithmetic and copies ran while one was open for 1% -> 1% of each run, Pallas kernels for 12% -> 11%
where the time goes in v3:
time: 85.6 us; the launch traced here: 85.4 us
  waiting for transfers between devices  36.7 us (43%)
  starting transfers between devices  34.1 us (40%)
  Pallas kernels  11.8 us (14%)
  between operations  1.51 us (2%)
  local copies, waits for them, and re-layouts  1.29 us (2%)
    ppermute x27, waiting for transfers between devices, swap(): lax.ppermute(x, AXES, [(i, i ^ (odd if i & 1 else even)) for i in range(c...  30.3 us
    ppermute x27, starting transfers between devices, swap(): lax.ppermute(x, AXES, [(i, i ^ (odd if i & 1 else even)) for i in range(c...  30.1 us
    pallas_call x33, Pallas kernels, call(): *got, self.token = kernel(*scalars, *from_hbm, *ins)  11.8 us
    all_to_all x1, waiting for transfers between devices, in_blocks(): squares = lax.all_to_all(squares, AXES, 0, 0, tiled=True)  6.39 us
    all_to_all x1, starting transfers between devices, in_blocks(): squares = lax.all_to_all(squares, AXES, 0, 0, tiled=True)  4.06 us
  transfers between devices with their start and end apart: 28, of which 13 were waited for; matrix products, arithmetic and copies ran while one was open for 1% of the time, Pallas kernels for 11%

profile of v3, /device:TPU:0, one launch (start us, length us, event | category | flops | bytes accessed | tf_op | source)
XLA Modules:
  0.0 85.4 jit_solution(3599832624854908208)
XLA Ops:
  1.3 0.7 copy-done.6
  2.0 0.1 shard_map.103
  2.1 0.5 collective-permute-start
  2.6 0.2 shard_map.104
  2.8 0.6 collective-permute-done.refs_1_
  3.4 2.9 %collective-permute-start.1 = (f32[8,128]{1,0:T(8,128)S(1)}, f32[8,128]{1,0:T(8,128)S(1)}, u32[]{:S(2)}, u32[]{:S(2)}) collective-permute-start(f32[8,128]{1,0:T(8,128)S(1)} %get-tuple-element.104.refs_0_), channel_id=1, source_target_pairs={{0,2},{1,3},{2,0},{3,1},{4,6},{5,7},{6,4},{7,5},{8,10},{9,11},{10,... | collective-permute-start | bytes 12296 | tf_op jit(solution)/shard_map/ppermute | solution.py:30
  6.3 1.3 %shard_map.106 = (f32[256,512]{1,0:T(8,128)S(1)}, f32[8,128]{1,0:T(8,128)S(1)}) custom-call(bf16[512,4096]{1,0:T(8,128)(2,1)S(1)} %bitcast.2, bf16[4096,256]{1,0:T(8,128)(2,1)S(1)} %copy-done.2, f32[8,128]{1,0:T(8,128)S(1)} %get-tuple-element.102.refs_2_), custom_call_target="tpu_custom_call" | custom-call | tf_op jit(solution)/shard_map/pallas_call | solution.py:68
  7.6 0.2 collective-permute-done.1.refs_1_
  7.9 2.1 %collective-permute-start.2 = (f32[8,128]{1,0:T(8,128)S(1)}, f32[8,128]{1,0:T(8,128)S(1)}, u32[]{:S(2)}, u32[]{:S(2)}) collective-permute-start(f32[8,128]{1,0:T(8,128)S(1)} %get-tuple-element.110.refs_4_), channel_id=1, source_target_pairs={{0,4},{1,5},{2,6},{3,7},{4,0},{5,1},{6,2},{7,3},{8,12},{9,13},{10,... | collective-permute-start | bytes 12296 | tf_op jit(solution)/shard_map/ppermute | solution.py:30
  10.0 1.3 %shard_map.108 = (f32[256,512]{1,0:T(8,128)S(1)}, f32[8,128]{1,0:T(8,128)S(1)}) custom-call(bf16[512,4096]{1,0:T(8,128)(2,1)S(1)} %bitcast.10, bf16[4096,256]{1,0:T(8,128)(2,1)S(1)} %copy-done.3, f32[8,128]{1,0:T(8,128)S(1)} %get-tuple-element.107.refs_2_), custom_call_target="tpu_custom_call" | custom-call | tf_op jit(solution)/shard_map/pallas_call | solution.py:68
  11.3 0.3 collective-permute-done.2.refs_5_
  11.6 0.2 shard_map.109
  11.8 0.5 shard_map.110
  12.3 0.1 collective-permute-start.3
  12.4 0.8 shard_map.111
  13.1 0.6 collective-permute-start.4
  13.7 0.6 collective-permute-done.3.refs_1_
  14.3 0.1 shard_map.112
  14.4 0.8 shard_map.113
  15.2 0.2 collective-permute-start.5
  15.5 0.8 shard_map.115
  16.3 0.4 collective-permute-start.6
  16.7 2.0 %collective-permute-start.8 = (f32[8,136,128]{2,1,0:T(8,128)S(1)}, f32[8,136,128]{2,1,0:T(8,128)S(1)}, u32[]{:S(2)}, u32[]{:S(2)}) collective-permute-start(f32[8,136,128]{2,1,0:T(8,128)S(1)} %get-tuple-element.137), channel_id=1, source_target_pairs={{0,4},{1,3},{2,6},{3,1},{4,0},{5,7},{6,2},{7,5},{8,12},{9,11},{10,... | collective-permute-start | bytes 1671176 | tf_op jit(solution)/shard_map/ppermute | solution.py:30
  18.7 0.1 shard_map.116
  18.8 0.5 shard_map.117
  19.3 0.1 shard_map.118
  19.4 1.4 %shard_map.119 = (f32[8,136,128]{2,1,0:T(8,128)S(1)}, f32[8,104,128]{2,1,0:T(8,128)S(1)}, f32[8,152,128]{2,1,0:T(8,128)S(1)}, f32[8,120,128]{2,1,0:T(8,128)S(1)}, f32[8,128]{1,0:T(8,128)S(1)}) custom-call(bf16[512,4096]{1,0:T(8,128)(2,1)S(1)} %bitcast.8, bf16[512,4096]{1,0:T(8,128)(2,1)S(1)} %bitcast.16, bf16[256,512]{1,0:T(8,128)(2,1)S(1)} %get-tuple-element.114.refs_2_, ...), custom_call_target="tpu_custom_call" | custom-call | tf_op jit(solution)/shard_map/pallas_call | solution.py:68
  20.8 0.1 collective-permute-start.7
  20.8 1.5 %collective-permute-start.15 = (f32[8,104,128]{2,1,0:T(8,128)S(1)}, f32[8,104,128]{2,1,0:T(8,128)S(1)}, u32[]{:S(2)}, u32[]{:S(2)}) collective-permute-start(f32[8,104,128]{2,1,0:T(8,128)S(1)} %get-tuple-element.149), channel_id=1, source_target_pairs={{0,2},{1,5},{2,0},{3,7},{4,6},{5,1},{6,4},{7,3},{8,10},{9,13},{10,... | collective-permute-start | bytes 1277960 | tf_op jit(solution)/shard_map/ppermute | solution.py:30
  22.4 1.6 %collective-permute-start.11 = (f32[8,152,128]{2,1,0:T(8,128)S(1)}, f32[8,152,128]{2,1,0:T(8,128)S(1)}, u32[]{:S(2)}, u32[]{:S(2)}) collective-permute-start(f32[8,152,128]{2,1,0:T(8,128)S(1)} %get-tuple-element.143), channel_id=1, source_target_pairs={{0,8},{1,9},{2,10},{3,11},{4,12},{5,13},{6,14},{7,15},{8,0},{9,1},... | collective-permute-start | bytes 1867784 | tf_op jit(solution)/shard_map/ppermute | solution.py:30
  24.0 6.2 %collective-permute-done.15.refs_2_ = f32[8,104,128]{2,1,0:T(8,128)S(1)} collective-permute-done((f32[8,104,128]{2,1,0:T(8,128)S(1)}, f32[8,104,128]{2,1,0:T(8,128)S(1)}, u32[]{:S(2)}, u32[]{:S(2)}) %collective-permute-start.15) | collective-permute-done | bytes 426016 | tf_op jit(solution)/shard_map/ppermute | solution.py:30
  30.2 1.7 %collective-permute-start.13 = (f32[8,120,128]{2,1,0:T(8,128)S(1)}, f32[8,120,128]{2,1,0:T(8,128)S(1)}, u32[]{:S(2)}, u32[]{:S(2)}) collective-permute-start(f32[8,120,128]{2,1,0:T(8,128)S(1)} %get-tuple-element.146), channel_id=1, source_target_pairs={{0,2},{1,5},{2,0},{3,7},{4,6},{5,1},{6,4},{7,3},{8,10},{9,13},{10,... | collective-permute-start | bytes 1474568 | tf_op jit(solution)/shard_map/ppermute | solution.py:30
  31.9 0.7 collective-permute-start.12
  32.7 0.1 collective-permute-start.14
  32.7 1.4 %shard_map.120 = (f32[8,136,128]{2,1,0:T(8,128)S(1)}, f32[8,104,128]{2,1,0:T(8,128)S(1)}, f32[8,152,128]{2,1,0:T(8,128)S(1)}, f32[8,120,128]{2,1,0:T(8,128)S(1)}, f32[8,128]{1,0:T(8,128)S(1)}) custom-call(bf16[512,4096]{1,0:T(8,128)(2,1)S(1)} %bitcast.9, bf16[512,4096]{1,0:T(8,128)(2,1)S(1)} %bitcast.17, bf16[256,512]{1,0:T(8,128)(2,1)S(1)} %get-tuple-element.114.refs_2_, ...), custom_call_target="tpu_custom_call" | custom-call | tf_op jit(solution)/shard_map/pallas_call | solution.py:68
  34.1 0.1 shard_map.121
  34.2 0.5 collective-permute-done.14.refs_1_
  34.8 0.1 shard_map.122
  34.8 4.2 %collective-permute-done.13.refs_2_ = f32[8,120,128]{2,1,0:T(8,128)S(1)} collective-permute-done((f32[8,120,128]{2,1,0:T(8,128)S(1)}, f32[8,120,128]{2,1,0:T(8,128)S(1)}, u32[]{:S(2)}, u32[]{:S(2)}) %collective-permute-start.13) | collective-permute-done | bytes 491552 | tf_op jit(solution)/shard_map/ppermute | solution.py:30
  39.0 0.1 shard_map.123
  39.1 0.1 shard_map.124
  39.2 1.9 %collective-permute-start.17 = (f32[4,152,128]{2,1,0:T(8,128)S(1)}, f32[4,152,128]{2,1,0:T(8,128)S(1)}, u32[]{:S(2)}, u32[]{:S(2)}) collective-permute-start(f32[4,152,128]{2,1,0:T(8,128)S(1)} %get-tuple-element.157), channel_id=1, source_target_pairs={{0,4},{1,3},{2,6},{3,1},{4,0},{5,7},{6,2},{7,5},{8,12},{9,11},{10,... | collective-permute-start | bytes 933896 | tf_op jit(solution)/shard_map/ppermute | solution.py:30
  41.1 1.5 %collective-permute-start.9 = (f32[4,136,128]{2,1,0:T(8,128)S(1)}, f32[4,136,128]{2,1,0:T(8,128)S(1)}, u32[]{:S(2)}, u32[]{:S(2)}) collective-permute-start(f32[4,136,128]{2,1,0:T(8,128)S(1)} %get-tuple-element.140), channel_id=1, source_target_pairs={{0,2},{1,5},{2,0},{3,7},{4,6},{5,1},{6,4},{7,3},{8,10},{9,13},{10,... | collective-permute-start | bytes 835592 | tf_op jit(solution)/shard_map/ppermute | solution.py:30
  42.6 0.5 collective-permute-start.18
  43.1 1.6 %collective-permute-start.19 = (f32[4,104,128]{2,1,0:T(8,128)S(1)}, f32[4,104,128]{2,1,0:T(8,128)S(1)}, u32[]{:S(2)}, u32[]{:S(2)}) collective-permute-start(f32[4,104,128]{2,1,0:T(8,128)S(1)} %get-tuple-element.161), channel_id=1, source_target_pairs={{0,8},{1,9},{2,10},{3,11},{4,12},{5,13},{6,14},{7,15},{8,0},{9,1},... | collective-permute-start | bytes 638984 | tf_op jit(solution)/shard_map/ppermute | solution.py:30
  44.7 6.0 %collective-permute-done.9.refs_1_ = f32[4,136,128]{2,1,0:T(8,128)S(1)} collective-permute-done((f32[4,136,128]{2,1,0:T(8,128)S(1)}, f32[4,136,128]{2,1,0:T(8,128)S(1)}, u32[]{:S(2)}, u32[]{:S(2)}) %collective-permute-start.9) | collective-permute-done | bytes 278560 | tf_op jit(solution)/shard_map/ppermute | solution.py:30
  50.7 1.1 %collective-permute-done.18.refs_1_ = f32[4,120,128]{2,1,0:T(8,128)S(1)} collective-permute-done((f32[4,120,128]{2,1,0:T(8,128)S(1)}, f32[4,120,128]{2,1,0:T(8,128)S(1)}, u32[]{:S(2)}, u32[]{:S(2)}) %collective-permute-start.18) | collective-permute-done | bytes 245792 | tf_op jit(solution)/shard_map/ppermute | solution.py:30
  51.9 1.0 %collective-permute-start.21 = (f32[2,152,128]{2,1,0:T(8,128)S(1)}, f32[2,152,128]{2,1,0:T(8,128)S(1)}, u32[]{:S(2)}, u32[]{:S(2)}) collective-permute-start(f32[2,152,128]{2,1,0:T(8,128)S(1)} %get-tuple-element.170), channel_id=1, source_target_pairs={{0,2},{1,5},{2,0},{3,7},{4,6},{5,1},{6,4},{7,3},{8,10},{9,13},{10,... | collective-permute-start | bytes 466952 | tf_op jit(solution)/shard_map/ppermute | solution.py:30
  52.9 1.8 %collective-permute-start.16 = (f32[2,136,128]{2,1,0:T(8,128)S(1)}, f32[2,136,128]{2,1,0:T(8,128)S(1)}, u32[]{:S(2)}, u32[]{:S(2)}) collective-permute-start(f32[2,136,128]{2,1,0:T(8,128)S(1)} %get-tuple-element.155), channel_id=1, source_target_pairs={{0,8},{1,9},{2,10},{3,11},{4,12},{5,13},{6,14},{7,15},{8,0},{9,1},... | collective-permute-start | bytes 417800 | tf_op jit(solution)/shard_map/ppermute | solution.py:30
  54.7 0.3 collective-permute-start.20
  55.0 2.8 %collective-permute-start.22 = (f32[2,104,128]{2,1,0:T(8,128)S(1)}, f32[2,104,128]{2,1,0:T(8,128)S(1)}, u32[]{:S(2)}, u32[]{:S(2)}) collective-permute-start(f32[2,104,128]{2,1,0:T(8,128)S(1)} %get-tuple-element.175), channel_id=1, source_target_pairs={{0,16},{1,17},{2,18},{3,19},{4,20},{5,21},{6,22},{7,23},{8,24},{9,... | collective-permute-start | bytes 319496 | tf_op jit(solution)/shard_map/ppermute | solution.py:30
  57.7 4.8 %collective-permute-done.16.refs_1_ = f32[2,136,128]{2,1,0:T(8,128)S(1)} collective-permute-done((f32[2,136,128]{2,1,0:T(8,128)S(1)}, f32[2,136,128]{2,1,0:T(8,128)S(1)}, u32[]{:S(2)}, u32[]{:S(2)}) %collective-permute-start.16) | collective-permute-done | bytes 139296 | tf_op jit(solution)/shard_map/ppermute | solution.py:30
  62.7 1.0 %collective-permute-start.26 = (f32[1,152,128]{2,1,0:T(8,128)S(1)}, f32[1,152,128]{2,1,0:T(8,128)S(1)}, u32[]{:S(2)}, u32[]{:S(2)}) collective-permute-start(f32[1,152,128]{2,1,0:T(8,128)S(1)} %get-tuple-element.182), channel_id=1, source_target_pairs={{0,16},{1,17},{2,18},{3,19},{4,20},{5,21},{6,22},{7,23},{8,24},{9,... | collective-permute-start | bytes 233480 | tf_op jit(solution)/shard_map/ppermute | solution.py:30
  63.6 2.0 %collective-permute-start.23 = (f32[1,136,128]{2,1,0:T(8,128)S(1)}, f32[1,136,128]{2,1,0:T(8,128)S(1)}, u32[]{:S(2)}, u32[]{:S(2)}) collective-permute-start(f32[1,136,128]{2,1,0:T(8,128)S(1)} %get-tuple-element.179), channel_id=1, source_target_pairs={{0,16},{1,17},{2,18},{3,19},{4,20},{5,21},{6,22},{7,23},{8,24},{9,... | collective-permute-start | bytes 208904 | tf_op jit(solution)/shard_map/ppermute | solution.py:30
  65.7 1.0 %collective-permute-start.24 = (f32[1,120,128]{2,1,0:T(8,128)S(1)}, f32[1,120,128]{2,1,0:T(8,128)S(1)}, u32[]{:S(2)}, u32[]{:S(2)}) collective-permute-start(f32[1,120,128]{2,1,0:T(8,128)S(1)} %get-tuple-element.180), channel_id=1, source_target_pairs={{0,16},{1,17},{2,18},{3,19},{4,20},{5,21},{6,22},{7,23},{8,24},{9,... | collective-permute-start | bytes 184328 | tf_op jit(solution)/shard_map/ppermute | solution.py:30
  66.6 0.4 collective-permute-start.25
  67.0 5.0 %collective-permute-done.23.refs_4_ = f32[1,136,128]{2,1,0:T(8,128)S(1)} collective-permute-done((f32[1,136,128]{2,1,0:T(8,128)S(1)}, f32[1,136,128]{2,1,0:T(8,128)S(1)}, u32[]{:S(2)}, u32[]{:S(2)}) %collective-permute-start.23) | collective-permute-done | bytes 69664 | tf_op jit(solution)/shard_map/ppermute | solution.py:30
  72.1 0.7 collective-permute-done.24.refs_5_
  72.7 0.7 shard_map.133
  73.4 4.1 %all-to-all-start = ((f32[32,1,128]{2,1,0:T(1,128)}), f32[32,1,128]{2,1,0:T(1,128)S(1)}, u32[]{:S(2)}, u32[]{:S(2)}) async-start(f32[32,1,128]{2,1,0:T(1,128)} %get-tuple-element.189), calls=%async_computation | async-start | bytes 32768 | tf_op jit(solution)/shard_map/all_to_all | solution.py:344
  77.5 0.6 copy.11
  78.1 0.1 shard_map.134
  78.2 6.4 %all-to-all-done.refs_2_ = f32[32,1,128]{2,1,0:T(1,128)S(1)} async-done(((f32[32,1,128]{2,1,0:T(1,128)}), f32[32,1,128]{2,1,0:T(1,128)S(1)}, u32[]{:S(2)}, u32[]{:S(2)}) %all-to-all-start) | async-done | bytes 16416 | tf_op jit(solution)/shard_map/all_to_all | solution.py:344
  84.6 0.8 shard_map.135
  (41 shorter events, 0.4 us)
Async XLA Ops:
  1.3 0.7 copy-start.6
  2.1 1.3 %collective-permute-start = (f32[8,128]{1,0:T(8,128)S(1)}, f32[8,128]{1,0:T(8,128)S(1)}, u32[]{:S(2)}, u32[]{:S(2)}) collective-permute-start(f32[8,128]{1,0:T(8,128)S(1)} %get-tuple-element.98.refs_0_), channel_id=1, source_target_pairs={{0,1},{1,0},{2,3},{3,2},{4,5},{5,4},{6,7},{7,6},{8,9},{9,8},{10,11... | collective-permute-start | bytes 12296 | tf_op jit(solution)/shard_map/ppermute | solution.py:30
  2.6 3.7 %copy-start = (bf16[1,512,4096]{2,1,0:T(8,128)(2,1)S(1)}, bf16[1,512,4096]{2,1,0:T(8,128)(2,1)}, u32[]{:S(2)}) copy-start(bf16[1,512,4096]{2,1,0:T(8,128)(2,1)} %param.8) | copy-start | bytes 12582916
  2.6 3.7 %copy-start.2 = (bf16[4096,256]{1,0:T(8,128)(2,1)S(1)}, bf16[4096,256]{1,0:T(8,128)(2,1)}, u32[]{:S(2)}) copy-start(bf16[4096,256]{1,0:T(8,128)(2,1)} %refs_1_.4) | copy-start | bytes 6291460
  2.8 7.2 %copy-start.1 = (bf16[1,512,4096]{2,1,0:T(8,128)(2,1)S(1)}, bf16[1,512,4096]{2,1,0:T(8,128)(2,1)}, u32[]{:S(2)}) copy-start(bf16[1,512,4096]{2,1,0:T(8,128)(2,1)} %param.9) | copy-start | bytes 12582916
  2.8 7.2 %copy-start.3 = (bf16[4096,256]{1,0:T(8,128)(2,1)S(1)}, bf16[4096,256]{1,0:T(8,128)(2,1)}, u32[]{:S(2)}) copy-start(bf16[4096,256]{1,0:T(8,128)(2,1)} %refs_1_.5) | copy-start | bytes 6291460
  3.4 4.5 %collective-permute-start.1 = (f32[8,128]{1,0:T(8,128)S(1)}, f32[8,128]{1,0:T(8,128)S(1)}, u32[]{:S(2)}, u32[]{:S(2)}) collective-permute-start(f32[8,128]{1,0:T(8,128)S(1)} %get-tuple-element.104.refs_0_), channel_id=1, source_target_pairs={{0,2},{1,3},{2,0},{3,1},{4,6},{5,7},{6,4},{7,5},{8,10},{9,11},{10,... | collective-permute-start | bytes 12296 | tf_op jit(solution)/shard_map/ppermute | solution.py:30
  7.6 4.0 %copy-start.4 = (f32[1,512]{1,0:T(1,128)S(1)}, f32[1,512]{1,0:T(1,128)}, u32[]{:S(2)}) copy-start(f32[1,512]{1,0:T(1,128)} %refs_7_.1) | copy-start | bytes 6148
  7.6 4.0 %copy-start.5 = (f32[1,512]{1,0:T(1,128)S(1)}, f32[1,512]{1,0:T(1,128)}, u32[]{:S(2)}) copy-start(f32[1,512]{1,0:T(1,128)} %refs_8_.1) | copy-start | bytes 6148
  7.9 3.7 %collective-permute-start.2 = (f32[8,128]{1,0:T(8,128)S(1)}, f32[8,128]{1,0:T(8,128)S(1)}, u32[]{:S(2)}, u32[]{:S(2)}) collective-permute-start(f32[8,128]{1,0:T(8,128)S(1)} %get-tuple-element.110.refs_4_), channel_id=1, source_target_pairs={{0,4},{1,5},{2,6},{3,7},{4,0},{5,1},{6,2},{7,3},{8,12},{9,13},{10,... | collective-permute-start | bytes 12296 | tf_op jit(solution)/shard_map/ppermute | solution.py:30
  12.3 2.0 %collective-permute-start.3 = (f32[8,136,128]{2,1,0:T(8,128)S(1)}, f32[8,136,128]{2,1,0:T(8,128)S(1)}, u32[]{:S(2)}, u32[]{:S(2)}) collective-permute-start(f32[8,136,128]{2,1,0:T(8,128)S(1)} %get-tuple-element.119), channel_id=1, source_target_pairs={{0,1},{1,0},{2,3},{3,2},{4,5},{5,4},{6,7},{7,6},{8,9},{9,8},{10,11... | collective-permute-start | bytes 1671176 | tf_op jit(solution)/shard_map/ppermute | solution.py:30
  13.1 2.3 %collective-permute-start.4 = (f32[8,104,128]{2,1,0:T(8,128)S(1)}, f32[8,104,128]{2,1,0:T(8,128)S(1)}, u32[]{:S(2)}, u32[]{:S(2)}) collective-permute-start(f32[8,104,128]{2,1,0:T(8,128)S(1)} %get-tuple-element.123), channel_id=1, source_target_pairs={{0,1},{1,0},{2,3},{3,2},{4,5},{5,4},{6,7},{7,6},{8,9},{9,8},{10,11... | collective-permute-start | bytes 1277960 | tf_op jit(solution)/shard_map/ppermute | solution.py:30
  15.2 3.5 %collective-permute-start.5 = (f32[8,152,128]{2,1,0:T(8,128)S(1)}, f32[8,152,128]{2,1,0:T(8,128)S(1)}, u32[]{:S(2)}, u32[]{:S(2)}) collective-permute-start(f32[8,152,128]{2,1,0:T(8,128)S(1)} %get-tuple-element.127), channel_id=1, source_target_pairs={{0,1},{1,0},{2,3},{3,2},{4,5},{5,4},{6,7},{7,6},{8,9},{9,8},{10,11... | collective-permute-start | bytes 1867784 | tf_op jit(solution)/shard_map/ppermute | solution.py:30
  16.3 3.0 %collective-permute-start.6 = (f32[8,120,128]{2,1,0:T(8,128)S(1)}, f32[8,120,128]{2,1,0:T(8,128)S(1)}, u32[]{:S(2)}, u32[]{:S(2)}) collective-permute-start(f32[8,120,128]{2,1,0:T(8,128)S(1)} %get-tuple-element.131), channel_id=1, source_target_pairs={{0,1},{1,0},{2,3},{3,2},{4,5},{5,4},{6,7},{7,6},{8,9},{9,8},{10,11... | collective-permute-start | bytes 1474568 | tf_op jit(solution)/shard_map/ppermute | solution.py:30
  16.7 15.2 %collective-permute-start.8 = (f32[8,136,128]{2,1,0:T(8,128)S(1)}, f32[8,136,128]{2,1,0:T(8,128)S(1)}, u32[]{:S(2)}, u32[]{:S(2)}) collective-permute-start(f32[8,136,128]{2,1,0:T(8,128)S(1)} %get-tuple-element.137), channel_id=1, source_target_pairs={{0,4},{1,3},{2,6},{3,1},{4,0},{5,7},{6,2},{7,5},{8,12},{9,11},{10,... | collective-permute-start | bytes 1671176 | tf_op jit(solution)/shard_map/ppermute | solution.py:30
  20.8 11.9 %collective-permute-start.7 = (f32[8,136,128]{2,1,0:T(8,128)S(1)}, f32[8,136,128]{2,1,0:T(8,128)S(1)}, u32[]{:S(2)}, u32[]{:S(2)}) collective-permute-start(f32[8,136,128]{2,1,0:T(8,128)S(1)} %get-tuple-element.136), channel_id=1, source_target_pairs={{0,1},{1,0},{2,3},{3,2},{4,5},{5,4},{6,7},{7,6},{8,9},{9,8},{10,11... | collective-permute-start | bytes 1671176 | tf_op jit(solution)/shard_map/ppermute | solution.py:30
  20.8 9.3 %collective-permute-start.15 = (f32[8,104,128]{2,1,0:T(8,128)S(1)}, f32[8,104,128]{2,1,0:T(8,128)S(1)}, u32[]{:S(2)}, u32[]{:S(2)}) collective-permute-start(f32[8,104,128]{2,1,0:T(8,128)S(1)} %get-tuple-element.149), channel_id=1, source_target_pairs={{0,2},{1,5},{2,0},{3,7},{4,6},{5,1},{6,4},{7,3},{8,10},{9,13},{10,... | collective-permute-start | bytes 1277960 | tf_op jit(solution)/shard_map/ppermute | solution.py:30
  22.4 16.7 %collective-permute-start.11 = (f32[8,152,128]{2,1,0:T(8,128)S(1)}, f32[8,152,128]{2,1,0:T(8,128)S(1)}, u32[]{:S(2)}, u32[]{:S(2)}) collective-permute-start(f32[8,152,128]{2,1,0:T(8,128)S(1)} %get-tuple-element.143), channel_id=1, source_target_pairs={{0,8},{1,9},{2,10},{3,11},{4,12},{5,13},{6,14},{7,15},{8,0},{9,1},... | collective-permute-start | bytes 1867784 | tf_op jit(solution)/shard_map/ppermute | solution.py:30
  24.0 15.2 %collective-permute-start.10 = (f32[8,152,128]{2,1,0:T(8,128)S(1)}, f32[8,152,128]{2,1,0:T(8,128)S(1)}, u32[]{:S(2)}, u32[]{:S(2)}) collective-permute-start(f32[8,152,128]{2,1,0:T(8,128)S(1)} %get-tuple-element.142), channel_id=1, source_target_pairs={{0,1},{1,0},{2,3},{3,2},{4,5},{5,4},{6,7},{7,6},{8,9},{9,8},{10,11... | collective-permute-start | bytes 1867784 | tf_op jit(solution)/shard_map/ppermute | solution.py:30
  30.2 8.8 %collective-permute-start.13 = (f32[8,120,128]{2,1,0:T(8,128)S(1)}, f32[8,120,128]{2,1,0:T(8,128)S(1)}, u32[]{:S(2)}, u32[]{:S(2)}) collective-permute-start(f32[8,120,128]{2,1,0:T(8,128)S(1)} %get-tuple-element.146), channel_id=1, source_target_pairs={{0,2},{1,5},{2,0},{3,7},{4,6},{5,1},{6,4},{7,3},{8,10},{9,13},{10,... | collective-permute-start | bytes 1474568 | tf_op jit(solution)/shard_map/ppermute | solution.py:30
  31.9 7.1 %collective-permute-start.12 = (f32[8,120,128]{2,1,0:T(8,128)S(1)}, f32[8,120,128]{2,1,0:T(8,128)S(1)}, u32[]{:S(2)}, u32[]{:S(2)}) collective-permute-start(f32[8,120,128]{2,1,0:T(8,128)S(1)} %get-tuple-element.145), channel_id=1, source_target_pairs={{0,1},{1,0},{2,3},{3,2},{4,5},{5,4},{6,7},{7,6},{8,9},{9,8},{10,11... | collective-permute-start | bytes 1474568 | tf_op jit(solution)/shard_map/ppermute | solution.py:30
  32.7 2.1 %collective-permute-start.14 = (f32[8,104,128]{2,1,0:T(8,128)S(1)}, f32[8,104,128]{2,1,0:T(8,128)S(1)}, u32[]{:S(2)}, u32[]{:S(2)}) collective-permute-start(f32[8,104,128]{2,1,0:T(8,128)S(1)} %get-tuple-element.148), channel_id=1, source_target_pairs={{0,1},{1,0},{2,3},{3,2},{4,5},{5,4},{6,7},{7,6},{8,9},{9,8},{10,11... | collective-permute-start | bytes 1277960 | tf_op jit(solution)/shard_map/ppermute | solution.py:30
  39.2 12.6 %collective-permute-start.17 = (f32[4,152,128]{2,1,0:T(8,128)S(1)}, f32[4,152,128]{2,1,0:T(8,128)S(1)}, u32[]{:S(2)}, u32[]{:S(2)}) collective-permute-start(f32[4,152,128]{2,1,0:T(8,128)S(1)} %get-tuple-element.157), channel_id=1, source_target_pairs={{0,4},{1,3},{2,6},{3,1},{4,0},{5,7},{6,2},{7,5},{8,12},{9,11},{10,... | collective-permute-start | bytes 933896 | tf_op jit(solution)/shard_map/ppermute | solution.py:30
  41.1 9.5 %collective-permute-start.9 = (f32[4,136,128]{2,1,0:T(8,128)S(1)}, f32[4,136,128]{2,1,0:T(8,128)S(1)}, u32[]{:S(2)}, u32[]{:S(2)}) collective-permute-start(f32[4,136,128]{2,1,0:T(8,128)S(1)} %get-tuple-element.140), channel_id=1, source_target_pairs={{0,2},{1,5},{2,0},{3,7},{4,6},{5,1},{6,4},{7,3},{8,10},{9,13},{10,... | collective-permute-start | bytes 835592 | tf_op jit(solution)/shard_map/ppermute | solution.py:30
  42.6 9.3 %collective-permute-start.18 = (f32[4,120,128]{2,1,0:T(8,128)S(1)}, f32[4,120,128]{2,1,0:T(8,128)S(1)}, u32[]{:S(2)}, u32[]{:S(2)}) collective-permute-start(f32[4,120,128]{2,1,0:T(8,128)S(1)} %get-tuple-element.159), channel_id=1, source_target_pairs={{0,4},{1,3},{2,6},{3,1},{4,0},{5,7},{6,2},{7,5},{8,12},{9,11},{10,... | collective-permute-start | bytes 737288 | tf_op jit(solution)/shard_map/ppermute | solution.py:30
  43.1 7.6 %collective-permute-start.19 = (f32[4,104,128]{2,1,0:T(8,128)S(1)}, f32[4,104,128]{2,1,0:T(8,128)S(1)}, u32[]{:S(2)}, u32[]{:S(2)}) collective-permute-start(f32[4,104,128]{2,1,0:T(8,128)S(1)} %get-tuple-element.161), channel_id=1, source_target_pairs={{0,8},{1,9},{2,10},{3,11},{4,12},{5,13},{6,14},{7,15},{8,0},{9,1},... | collective-permute-start | bytes 638984 | tf_op jit(solution)/shard_map/ppermute | solution.py:30
  51.9 10.7 %collective-permute-start.21 = (f32[2,152,128]{2,1,0:T(8,128)S(1)}, f32[2,152,128]{2,1,0:T(8,128)S(1)}, u32[]{:S(2)}, u32[]{:S(2)}) collective-permute-start(f32[2,152,128]{2,1,0:T(8,128)S(1)} %get-tuple-element.170), channel_id=1, source_target_pairs={{0,2},{1,5},{2,0},{3,7},{4,6},{5,1},{6,4},{7,3},{8,10},{9,13},{10,... | collective-permute-start | bytes 466952 | tf_op jit(solution)/shard_map/ppermute | solution.py:30
  52.9 9.7 %collective-permute-start.16 = (f32[2,136,128]{2,1,0:T(8,128)S(1)}, f32[2,136,128]{2,1,0:T(8,128)S(1)}, u32[]{:S(2)}, u32[]{:S(2)}) collective-permute-start(f32[2,136,128]{2,1,0:T(8,128)S(1)} %get-tuple-element.155), channel_id=1, source_target_pairs={{0,8},{1,9},{2,10},{3,11},{4,12},{5,13},{6,14},{7,15},{8,0},{9,1},... | collective-permute-start | bytes 417800 | tf_op jit(solution)/shard_map/ppermute | solution.py:30
  54.7 10.9 %collective-permute-start.20 = (f32[2,120,128]{2,1,0:T(8,128)S(1)}, f32[2,120,128]{2,1,0:T(8,128)S(1)}, u32[]{:S(2)}, u32[]{:S(2)}) collective-permute-start(f32[2,120,128]{2,1,0:T(8,128)S(1)} %get-tuple-element.168), channel_id=1, source_target_pairs={{0,8},{1,9},{2,10},{3,11},{4,12},{5,13},{6,14},{7,15},{8,0},{9,1},... | collective-permute-start | bytes 368648 | tf_op jit(solution)/shard_map/ppermute | solution.py:30
  55.0 11.7 %collective-permute-start.22 = (f32[2,104,128]{2,1,0:T(8,128)S(1)}, f32[2,104,128]{2,1,0:T(8,128)S(1)}, u32[]{:S(2)}, u32[]{:S(2)}) collective-permute-start(f32[2,104,128]{2,1,0:T(8,128)S(1)} %get-tuple-element.175), channel_id=1, source_target_pairs={{0,16},{1,17},{2,18},{3,19},{4,20},{5,21},{6,22},{7,23},{8,24},{9,... | collective-permute-start | bytes 319496 | tf_op jit(solution)/shard_map/ppermute | solution.py:30
  62.7 10.1 %collective-permute-start.26 = (f32[1,152,128]{2,1,0:T(8,128)S(1)}, f32[1,152,128]{2,1,0:T(8,128)S(1)}, u32[]{:S(2)}, u32[]{:S(2)}) collective-permute-start(f32[1,152,128]{2,1,0:T(8,128)S(1)} %get-tuple-element.182), channel_id=1, source_target_pairs={{0,16},{1,17},{2,18},{3,19},{4,20},{5,21},{6,22},{7,23},{8,24},{9,... | collective-permute-start | bytes 233480 | tf_op jit(solution)/shard_map/ppermute | solution.py:30
  63.6 8.5 %collective-permute-start.23 = (f32[1,136,128]{2,1,0:T(8,128)S(1)}, f32[1,136,128]{2,1,0:T(8,128)S(1)}, u32[]{:S(2)}, u32[]{:S(2)}) collective-permute-start(f32[1,136,128]{2,1,0:T(8,128)S(1)} %get-tuple-element.179), channel_id=1, source_target_pairs={{0,16},{1,17},{2,18},{3,19},{4,20},{5,21},{6,22},{7,23},{8,24},{9,... | collective-permute-start | bytes 208904 | tf_op jit(solution)/shard_map/ppermute | solution.py:30
  65.7 7.1 %collective-permute-start.24 = (f32[1,120,128]{2,1,0:T(8,128)S(1)}, f32[1,120,128]{2,1,0:T(8,128)S(1)}, u32[]{:S(2)}, u32[]{:S(2)}) collective-permute-start(f32[1,120,128]{2,1,0:T(8,128)S(1)} %get-tuple-element.180), channel_id=1, source_target_pairs={{0,16},{1,17},{2,18},{3,19},{4,20},{5,21},{6,22},{7,23},{8,24},{9,... | collective-permute-start | bytes 184328 | tf_op jit(solution)/shard_map/ppermute | solution.py:30
  66.6 5.4 %collective-permute-start.25 = (f32[1,104,128]{2,1,0:T(8,128)S(1)}, f32[1,104,128]{2,1,0:T(8,128)S(1)}, u32[]{:S(2)}, u32[]{:S(2)}) collective-permute-start(f32[1,104,128]{2,1,0:T(8,128)S(1)} %get-tuple-element.181), channel_id=1, source_target_pairs={{0,4},{1,3},{2,6},{3,1},{4,0},{5,7},{6,2},{7,5},{8,12},{9,11},{10,... | collective-permute-start | bytes 159752 | tf_op jit(solution)/shard_map/ppermute | solution.py:30
  73.4 11.2 %all-to-all-start = ((f32[32,1,128]{2,1,0:T(1,128)}), f32[32,1,128]{2,1,0:T(1,128)S(1)}, u32[]{:S(2)}, u32[]{:S(2)}) async-start(f32[32,1,128]{2,1,0:T(1,128)} %get-tuple-element.189), calls=%async_computation | async-start | bytes 32768 | tf_op jit(solution)/shard_map/all_to_all | solution.py:344
